TPU v7x, 32 devices: a whole 2x2x4 slice. The times are simulated.
32 devices in a mesh: tm: 8 (over y, x, core), space: 4 (over z).
Axes of the slice: x: 2, y: 2, z: 4, core: 2. Of those that a mesh axis runs over, the one named last changes fastest.
Arguments:
- previous_end: float32 [8, 16, 256, 256], P('tm', 'space'), may hold values from -6 to 6
- source: float32 [8, 16, 256, 256], P('tm', 'space'), may hold values from -4 to 4
- rate: float32 [16, 256, 256], P('space'), may hold values from 0.05 to 0.8
Outputs:
- fine_nodes: float32 [8, 2, 16, 256, 256], P('tm', None, 'space')
All inputs are finite; a program needn't handle non-finite values.
Results may differ from a plain program's by a relative error of at most 0.00026.
Values sent between devices are 32-bit elements; how exact they have to be, the bound alone decides.
A program may use at most 128 MiB of HBM per device.

v0:
```python
import jax
import jax.numpy as jnp
from jax import lax
from jax.sharding import PartitionSpec as P

diffusion = 0.1
speed_z = 0.4
speed_x = 0.3
speed_y = 0.2
weights_one = (5.0 / 24.0, 1.0 / 3.0, -1.0 / 24.0)
weights_two = (-1.0 / 24.0, 1.0 / 3.0, 5.0 / 24.0)


def broadcast(array, axis, root):
    mine = lax.axis_index(axis) == root
    return lax.psum(jnp.where(mine, array, jnp.zeros_like(array)), axis)


def padded_2(array, sides, width):
    for axis, dim in sides:
        size, length = (lax.axis_size(axis), array.shape[dim])
        up = [(i, (i + 1) % size) for i in range(size - 1)]
        down = [(j, i) for i, j in up]
        last = lax.slice_in_dim(array, length - width, length, axis=dim)
        first = lax.slice_in_dim(array, 0, width, axis=dim)
        before = lax.ppermute(last, axis, up)
        after = lax.ppermute(first, axis, down)
        array = jnp.concatenate([before, array, after], axis=dim)
    return array


def shifted(value, axis, steps):
    count = lax.axis_size(axis)
    first, last = (max(0, -steps), min(count, count - steps))
    return lax.ppermute(value, axis, [(source, source + steps) for source in range(first, last)])


def tendency(padded, rate_field, source_term, spacing):
    middle = padded[..., 1:-1, :, :]
    upper_z = padded[..., 2:, :, :]
    lower_z = padded[..., :-2, :, :]
    plus_x = jnp.roll(middle, -1, axis=-2)
    minus_x = jnp.roll(middle, 1, axis=-2)
    plus_y = jnp.roll(middle, -1, axis=-1)
    minus_y = jnp.roll(middle, 1, axis=-1)
    laplacian = (upper_z + lower_z + plus_x + minus_x + plus_y + minus_y - 6.0 * middle) / (
        spacing * spacing
    )
    transport = (
        speed_z * (upper_z - lower_z) + speed_x * (plus_x - minus_x) + speed_y * (plus_y - minus_y)
    ) / (2.0 * spacing)
    return (
        diffusion * laplacian
        - transport
        + rate_field * middle / (1.0 + middle * middle)
        + source_term
    )


def pair_table(count):
    fine_index = jnp.arange(count, dtype=jnp.int32)[:, None]
    coarse_index = jnp.arange(count // 2, dtype=jnp.int32)[None, :]
    return (fine_index // 2 == coarse_index).astype(jnp.float32)


def restrict(field):
    count_z, count_x, count_y = field.shape[-3:]
    paired = field.reshape(field.shape[:-3] + (count_z // 2, 2, count_x, count_y))
    summed_z = paired[..., 0, :, :] + paired[..., 1, :, :]
    summed_y = jnp.einsum(
        "...xy,yb->...xb", summed_z, pair_table(count_y), precision=lax.Precision.HIGHEST
    )
    summed_x = jnp.einsum(
        "...xb,xa->...ab", summed_y, pair_table(count_x), precision=lax.Precision.HIGHEST
    )
    return 0.125 * summed_x


def inject(coarse):
    count_x, count_y = coarse.shape[-2:]
    along_y = jnp.einsum(
        "...ab,yb->...ay", coarse, pair_table(2 * count_y), precision=lax.Precision.HIGHEST
    )
    along_x = jnp.einsum(
        "...ay,xa->...xy", along_y, pair_table(2 * count_x), precision=lax.Precision.HIGHEST
    )
    return jnp.repeat(along_x, 2, axis=-3)


def pick(stacked, index):
    return lax.dynamic_index_in_dim(stacked, index, 0, keepdims=False)


def broadcast_seed(warm):
    return broadcast(warm, "tm", lax.axis_size("tm") - 1)


def widen(stacked):
    return padded_2(stacked, (("space", 1),), 1)


def coarse_deep(start, rate_c, source_c, rate_wide, source_wide):
    padded = padded_2(start, (("space", 0),), 2)
    first_wide = padded[1:-1] + 0.5 * tendency(padded, rate_wide, source_wide, 2.0)
    count_z = start.shape[0]
    global_z = lax.axis_index("space") * count_z - 1 + jnp.arange(count_z + 2, dtype=jnp.int32)
    inside = (global_z >= 0) & (global_z < count_z * lax.axis_size("space"))
    first_wide = jnp.where(inside[:, None, None], first_wide, 0.0)
    second = first_wide[1:-1] + 0.5 * tendency(first_wide, rate_c, source_c, 2.0)
    return (first_wide[1:-1], second)


def coarse_pair(start, stacked, wide, index):
    return coarse_deep(start, stacked[0], pick(stacked, index), wide[0], pick(wide, index))


def shards(previous_end, source, rate):
    warm = previous_end[0]
    own_source = source[0]
    rank = lax.axis_index("tm")
    turns = lax.axis_size("tm") - 1
    rate_c = restrict(rate)
    source_c = restrict(own_source)
    stacked = jnp.stack([rate_c, source_c])
    wide = widen(stacked)
    restart = broadcast_seed(warm)
    restart_c = restrict(restart)

    def turn(step, value):
        first, second = coarse_pair(value, stacked, wide, 1)
        moved = shifted(second, "tm", 1)
        return jnp.where(rank == 0, restart_c, moved)

    start = lax.fori_loop(0, turns, turn, restart_c)
    first, second = coarse_pair(start, stacked, wide, 1)
    warm_c = restrict(warm)
    guess = jnp.stack(
        [
            restart + inject(start - restart_c),
            warm + inject(first - warm_c),
            warm + inject(second - warm_c),
        ]
    )
    padded = padded_2(guess, (("space", 1),), 1)
    images = tendency(padded, rate, own_source, 1.0)
    node_one = guess[0] + (
        weights_one[0] * images[0] + weights_one[1] * images[1] + weights_one[2] * images[2]
    )
    padded_one = padded_2(node_one, (("space", 0),), 1)
    again = tendency(padded_one, rate, own_source, 1.0)
    node_two = (
        node_one
        + 0.5 * (again - images[1])
        + (weights_two[0] * images[0] + weights_two[1] * images[1] + weights_two[2] * images[2])
    )
    return jnp.stack([node_one, node_two])[None]


def solution(mesh):
    placed = (P("tm", "space", None, None), P("tm", "space", None, None), P("space", None, None))
    return jax.shard_map(
        shards,
        mesh=mesh,
        in_specs=placed,
        out_specs=P("tm", None, "space", None, None),
        check_vma=False,
    )
```

profile of v0, /device:TPU:2, one launch (start us, length us, event | category | flops | bytes accessed | tf_op | source)
XLA Modules:
  0.0 267.3 jit_solution(10038256187280063621)
XLA Ops:
  6.5 1.7 fusion.18
  8.7 1.7 fusion.22
  10.7 3.5 %collective-permute-start.3 = (f32[2,1,128,128]{3,2,1,0:T(8,128)S(1)}, f32[2,1,128,128]{3,2,1,0:T(8,128)S(1)}, u32[]{:S(2)}, u32[]{:S(2)}) collective-permute-start(f32[2,1,128,128]{3,2,1,0:T(8,128)S(1)} %get-tuple-element.197), channel_id=1, source_target_pairs={{0,1},{1,2},{2,3},{4,5},{5,6},{6,7},{8,9},{9,10},{10,11},{12,13},{... | collective-permute-start | bytes 393224 | tf_op jit(solution)/shard_map/ppermute | solution.py:26
  18.2 2.9 %collective-permute-done.4 = f32[2,1,128,128]{3,2,1,0:T(8,128)S(1)} collective-permute-done((f32[2,1,128,128]{3,2,1,0:T(8,128)S(1)}, f32[2,1,128,128]{3,2,1,0:T(8,128)S(1)}, u32[]{:S(2)}, u32[]{:S(2)}) %collective-permute-start.4) | collective-permute-done | bytes 131104 | tf_op jit(solution)/shard_map/ppermute | solution.py:27
  21.1 53.8 %all-reduce.2.cloned.1.call-done = f32[4,256,256]{2,1,0:T(8,128)} async-done(((f32[4,256,256]{2,1,0:T(8,128)}), f32[4,256,256]{2,1,0:T(8,128)}) %all-reduce.2.cloned.1.call-update) | async-done | bytes 1048592 | tf_op jit(solution)/shard_map/psum | solution.py:16
  77.0 122.6 %while.13 = (s32[]{:T(128)}, f32[2,128,128]{2,1,0:T(8,128)S(1)}, pred[]{:T(512)}, f32[2,4,128,128]{3,2,1,0:T(8,128)S(1)}, f32[2,128,128]{2,1,0:T(8,128)S(1)}, /*...) while((s32[]{:T(128)}, f32[2,128,128]{2,1,0:T(8,128)S(1)}, ...), condition=%wide.region_2.3_spmd, body=%wide.region_1.2_spmd.sunk | while | flops 3047446 | bytes 10354974 | solution.py:134
  77.0 3.5 %collective-permute-start = (f32[2,128,128]{2,1,0:T(8,128)S(1)}, f32[2,128,128]{2,1,0:T(8,128)S(1)}, u32[]{:S(2)}, u32[]{:S(2)}) collective-permute-start(f32[2,128,128]{2,1,0:T(8,128)S(1)} %get-tuple-element.307), channel_id=1, source_target_pairs={{0,1},{1,2},{2,3},{4,5},{5,6},{6,7},{8,9},{9,10},{10,11},{12,13},{... | collective-permute-start | bytes 393224 | tf_op jit(solution)/shard_map/while/body/eval_jaxpr/ppermute | solution.py:26
  83.1 4.3 %collective-permute-done.1 = f32[2,128,128]{2,1,0:T(8,128)S(1)} collective-permute-done((f32[2,128,128]{2,1,0:T(8,128)S(1)}, f32[2,128,128]{2,1,0:T(8,128)S(1)}, u32[]{:S(2)}, u32[]{:S(2)}) %collective-permute-start.1) | collective-permute-done | bytes 131104 | tf_op jit(solution)/shard_map/while/body/eval_jaxpr/ppermute | solution.py:27
  88.6 1.9 collective-permute-start.2
  90.5 4.4 %collective-permute-done.2 = f32[2,128,128]{2,1,0:T(8,128)S(1)} collective-permute-done((f32[2,128,128]{2,1,0:T(8,128)S(1)}, f32[2,128,128]{2,1,0:T(8,128)S(1)}, u32[]{:S(2)}, u32[]{:S(2)}) %collective-permute-start.2) | collective-permute-done | bytes 131104 | tf_op jit(solution)/shard_map/while/body/eval_jaxpr/ppermute | solution.py:35
  94.9 3.4 %collective-permute-start = (f32[2,128,128]{2,1,0:T(8,128)S(1)}, f32[2,128,128]{2,1,0:T(8,128)S(1)}, u32[]{:S(2)}, u32[]{:S(2)}) collective-permute-start(f32[2,128,128]{2,1,0:T(8,128)S(1)} %get-tuple-element.307), channel_id=1, source_target_pairs={{0,1},{1,2},{2,3},{4,5},{5,6},{6,7},{8,9},{9,10},{10,11},{12,13},{... | collective-permute-start | bytes 393224 | tf_op jit(solution)/shard_map/while/body/eval_jaxpr/ppermute | solution.py:26
  100.9 4.3 %collective-permute-done.1 = f32[2,128,128]{2,1,0:T(8,128)S(1)} collective-permute-done((f32[2,128,128]{2,1,0:T(8,128)S(1)}, f32[2,128,128]{2,1,0:T(8,128)S(1)}, u32[]{:S(2)}, u32[]{:S(2)}) %collective-permute-start.1) | collective-permute-done | bytes 131104 | tf_op jit(solution)/shard_map/while/body/eval_jaxpr/ppermute | solution.py:27
  106.4 1.9 collective-permute-start.2
  108.3 4.4 %collective-permute-done.2 = f32[2,128,128]{2,1,0:T(8,128)S(1)} collective-permute-done((f32[2,128,128]{2,1,0:T(8,128)S(1)}, f32[2,128,128]{2,1,0:T(8,128)S(1)}, u32[]{:S(2)}, u32[]{:S(2)}) %collective-permute-start.2) | collective-permute-done | bytes 131104 | tf_op jit(solution)/shard_map/while/body/eval_jaxpr/ppermute | solution.py:35
  112.7 3.4 %collective-permute-start = (f32[2,128,128]{2,1,0:T(8,128)S(1)}, f32[2,128,128]{2,1,0:T(8,128)S(1)}, u32[]{:S(2)}, u32[]{:S(2)}) collective-permute-start(f32[2,128,128]{2,1,0:T(8,128)S(1)} %get-tuple-element.307), channel_id=1, source_target_pairs={{0,1},{1,2},{2,3},{4,5},{5,6},{6,7},{8,9},{9,10},{10,11},{12,13},{... | collective-permute-start | bytes 393224 | tf_op jit(solution)/shard_map/while/body/eval_jaxpr/ppermute | solution.py:26
  119.1 4.1 %collective-permute-done.1 = f32[2,128,128]{2,1,0:T(8,128)S(1)} collective-permute-done((f32[2,128,128]{2,1,0:T(8,128)S(1)}, f32[2,128,128]{2,1,0:T(8,128)S(1)}, u32[]{:S(2)}, u32[]{:S(2)}) %collective-permute-start.1) | collective-permute-done | bytes 131104 | tf_op jit(solution)/shard_map/while/body/eval_jaxpr/ppermute | solution.py:27
  124.4 1.9 collective-permute-start.2
  126.3 4.4 %collective-permute-done.2 = f32[2,128,128]{2,1,0:T(8,128)S(1)} collective-permute-done((f32[2,128,128]{2,1,0:T(8,128)S(1)}, f32[2,128,128]{2,1,0:T(8,128)S(1)}, u32[]{:S(2)}, u32[]{:S(2)}) %collective-permute-start.2) | collective-permute-done | bytes 131104 | tf_op jit(solution)/shard_map/while/body/eval_jaxpr/ppermute | solution.py:35
  130.7 2.2 collective-permute-start
  134.2 2.0 collective-permute-done
  136.3 4.1 %collective-permute-done.1 = f32[2,128,128]{2,1,0:T(8,128)S(1)} collective-permute-done((f32[2,128,128]{2,1,0:T(8,128)S(1)}, f32[2,128,128]{2,1,0:T(8,128)S(1)}, u32[]{:S(2)}, u32[]{:S(2)}) %collective-permute-start.1) | collective-permute-done | bytes 131104 | tf_op jit(solution)/shard_map/while/body/eval_jaxpr/ppermute | solution.py:27
  141.6 1.9 collective-permute-start.2
  143.5 4.4 %collective-permute-done.2 = f32[2,128,128]{2,1,0:T(8,128)S(1)} collective-permute-done((f32[2,128,128]{2,1,0:T(8,128)S(1)}, f32[2,128,128]{2,1,0:T(8,128)S(1)}, u32[]{:S(2)}, u32[]{:S(2)}) %collective-permute-start.2) | collective-permute-done | bytes 131104 | tf_op jit(solution)/shard_map/while/body/eval_jaxpr/ppermute | solution.py:35
  147.9 2.2 collective-permute-start
  151.4 2.0 collective-permute-done
  153.5 4.1 %collective-permute-done.1 = f32[2,128,128]{2,1,0:T(8,128)S(1)} collective-permute-done((f32[2,128,128]{2,1,0:T(8,128)S(1)}, f32[2,128,128]{2,1,0:T(8,128)S(1)}, u32[]{:S(2)}, u32[]{:S(2)}) %collective-permute-start.1) | collective-permute-done | bytes 131104 | tf_op jit(solution)/shard_map/while/body/eval_jaxpr/ppermute | solution.py:27
  158.8 1.9 collective-permute-start.2
  160.7 4.4 %collective-permute-done.2 = f32[2,128,128]{2,1,0:T(8,128)S(1)} collective-permute-done((f32[2,128,128]{2,1,0:T(8,128)S(1)}, f32[2,128,128]{2,1,0:T(8,128)S(1)}, u32[]{:S(2)}, u32[]{:S(2)}) %collective-permute-start.2) | collective-permute-done | bytes 131104 | tf_op jit(solution)/shard_map/while/body/eval_jaxpr/ppermute | solution.py:35
  165.1 2.2 collective-permute-start
  168.6 2.0 collective-permute-done
  170.7 4.1 %collective-permute-done.1 = f32[2,128,128]{2,1,0:T(8,128)S(1)} collective-permute-done((f32[2,128,128]{2,1,0:T(8,128)S(1)}, f32[2,128,128]{2,1,0:T(8,128)S(1)}, u32[]{:S(2)}, u32[]{:S(2)}) %collective-permute-start.1) | collective-permute-done | bytes 131104 | tf_op jit(solution)/shard_map/while/body/eval_jaxpr/ppermute | solution.py:27
  176.0 1.9 collective-permute-start.2
  177.9 4.4 %collective-permute-done.2 = f32[2,128,128]{2,1,0:T(8,128)S(1)} collective-permute-done((f32[2,128,128]{2,1,0:T(8,128)S(1)}, f32[2,128,128]{2,1,0:T(8,128)S(1)}, u32[]{:S(2)}, u32[]{:S(2)}) %collective-permute-start.2) | collective-permute-done | bytes 131104 | tf_op jit(solution)/shard_map/while/body/eval_jaxpr/ppermute | solution.py:35
  182.3 2.2 collective-permute-start
  185.9 2.0 collective-permute-done
  188.0 4.1 %collective-permute-done.1 = f32[2,128,128]{2,1,0:T(8,128)S(1)} collective-permute-done((f32[2,128,128]{2,1,0:T(8,128)S(1)}, f32[2,128,128]{2,1,0:T(8,128)S(1)}, u32[]{:S(2)}, u32[]{:S(2)}) %collective-permute-start.1) | collective-permute-done | bytes 131104 | tf_op jit(solution)/shard_map/while/body/eval_jaxpr/ppermute | solution.py:27
  193.2 1.9 collective-permute-start.2
  195.2 4.4 %collective-permute-done.2 = f32[2,128,128]{2,1,0:T(8,128)S(1)} collective-permute-done((f32[2,128,128]{2,1,0:T(8,128)S(1)}, f32[2,128,128]{2,1,0:T(8,128)S(1)}, u32[]{:S(2)}, u32[]{:S(2)}) %collective-permute-start.2) | collective-permute-done | bytes 131104 | tf_op jit(solution)/shard_map/while/body/eval_jaxpr/ppermute | solution.py:35
  201.2 4.6 %collective-permute-start.5 = (f32[2,128,128]{2,1,0:T(8,128)S(1)}, f32[2,128,128]{2,1,0:T(8,128)S(1)}, u32[]{:S(2)}, u32[]{:S(2)}) collective-permute-start(f32[2,128,128]{2,1,0:T(8,128)S(1)} %get-tuple-element.121), channel_id=1, source_target_pairs={{0,1},{1,2},{2,3},{4,5},{5,6},{6,7},{8,9},{9,10},{10,11},{12,13},{... | collective-permute-start | bytes 393224 | tf_op jit(solution)/shard_map/ppermute | solution.py:26
  206.3 2.8 %collective-permute-done.5 = f32[2,128,128]{2,1,0:T(8,128)S(1)} collective-permute-done((f32[2,128,128]{2,1,0:T(8,128)S(1)}, f32[2,128,128]{2,1,0:T(8,128)S(1)}, u32[]{:S(2)}, u32[]{:S(2)}) %collective-permute-start.5) | collective-permute-done | bytes 131104 | tf_op jit(solution)/shard_map/ppermute | solution.py:26
  213.5 4.4 %collective-permute-start.8 = (f32[3,1,256,256]{3,2,1,0:T(8,128)S(1)}, f32[3,1,256,256]{3,2,1,0:T(8,128)S(1)}, u32[]{:S(2)}, u32[]{:S(2)}) collective-permute-start(f32[3,1,256,256]{3,2,1,0:T(8,128)S(1)} %get-tuple-element.159), channel_id=1, source_target_pairs={{0,1},{1,2},{2,3},{4,5},{5,6},{6,7},{8,9},{9,10},{10,11},{12,13},{... | collective-permute-start | bytes 2359304 | tf_op jit(solution)/shard_map/ppermute | solution.py:26
  222.1 12.3 %collective-permute-done.8 = f32[3,1,256,256]{3,2,1,0:T(8,128)S(1)} collective-permute-done((f32[3,1,256,256]{3,2,1,0:T(8,128)S(1)}, f32[3,1,256,256]{3,2,1,0:T(8,128)S(1)}, u32[]{:S(2)}, u32[]{:S(2)}) %collective-permute-start.8) | collective-permute-done | bytes 786464 | tf_op jit(solution)/shard_map/ppermute | solution.py:26
  234.4 4.2 %collective-permute-done.7 = f32[3,1,256,256]{3,2,1,0:T(8,128)S(1)} collective-permute-done((f32[3,1,256,256]{3,2,1,0:T(8,128)S(1)}, f32[3,1,256,256]{3,2,1,0:T(8,128)S(1)}, u32[]{:S(2)}, u32[]{:S(2)}) %collective-permute-start.7) | collective-permute-done | bytes 786464 | tf_op jit(solution)/shard_map/ppermute | solution.py:27
  239.5 6.1 %add_add_fusion = f32[3,4,256,256]{3,2,1,0:T(8,128)S(1)} fusion(f32[3,4,256,255]{3,2,1,0:T(8,128)S(1)} %get-tuple-element.166, f32[3,4,256,1]{3,2,1,0:T(8,128)} %get-tuple-element.168, f32[3,4,256,1]{3,2,1,0:T(8,128)S(1)} %get-tuple-element.167, f32[3,4,256,255]{3,2,1,0:T(8,128)S(1)} %get-tuple-element.165, f32[3,4,255,256]{3,2,1,0:T(8,128)S(1)} %get-tuple-element.162, ...), kind=kLoop, calls=%fused_computation.38 | loop fusion | flops 28311552 | bytes 22544384 | tf_op jit(solution)/shard_map/add | solution.py:53
  246.4 2.2 collective-permute-start.10
  250.1 2.7 %collective-permute-done.10 = f32[1,256,256]{2,1,0:T(8,128)S(1)} collective-permute-done((f32[1,256,256]{2,1,0:T(8,128)S(1)}, f32[1,256,256]{2,1,0:T(8,128)S(1)}, u32[]{:S(2)}, u32[]{:S(2)}) %collective-permute-start.10) | collective-permute-done | bytes 262176 | tf_op jit(solution)/shard_map/ppermute | solution.py:26
  252.8 4.1 %collective-permute-done.9 = f32[1,256,256]{2,1,0:T(8,128)S(1)} collective-permute-done((f32[1,256,256]{2,1,0:T(8,128)S(1)}, f32[1,256,256]{2,1,0:T(8,128)S(1)}, u32[]{:S(2)}, u32[]{:S(2)}) %collective-permute-start.9) | collective-permute-done | bytes 262176 | tf_op jit(solution)/shard_map/ppermute | solution.py:27
  256.9 2.0 fusion.10
  (189 shorter events, 43.3 us)
Async XLA Ops:
  6.5 9.0 %copy-start = (f32[1,4,256,256]{3,2,1,0:T(8,128)S(1)}, f32[1,4,256,256]{3,2,1,0:T(8,128)}, u32[]{:S(2)}) copy-start(f32[1,4,256,256]{3,2,1,0:T(8,128)} %param.5) | copy-start | bytes 3145732
  6.5 68.4 %all-reduce.2.cloned.1.call-start = ((), (), s32[]{:S(2)}) async-start(), calls=%async_computation | async-start | bytes 2097152 | tf_op jit(solution)/shard_map/psum | solution.py:16
  8.6 12.5 %copy-start.4 = (f32[128,2,128]{2,0,1:T(8,128)}, f32[128,2,128]{2,0,1:T(8,128)S(1)}, u32[]{:S(2)}) copy-start(f32[128,2,128]{2,0,1:T(8,128)S(1)} %convolution_multiply_fusion.1) | copy-start | bytes 393220
  10.7 7.4 %collective-permute-start.3 = (f32[2,1,128,128]{3,2,1,0:T(8,128)S(1)}, f32[2,1,128,128]{3,2,1,0:T(8,128)S(1)}, u32[]{:S(2)}, u32[]{:S(2)}) collective-permute-start(f32[2,1,128,128]{3,2,1,0:T(8,128)S(1)} %get-tuple-element.197), channel_id=1, source_target_pairs={{0,1},{1,2},{2,3},{4,5},{5,6},{6,7},{8,9},{9,10},{10,11},{12,13},{... | collective-permute-start | bytes 393224 | tf_op jit(solution)/shard_map/ppermute | solution.py:26
  14.2 6.9 %collective-permute-start.4 = (f32[2,1,128,128]{3,2,1,0:T(8,128)S(1)}, f32[2,1,128,128]{3,2,1,0:T(8,128)S(1)}, u32[]{:S(2)}, u32[]{:S(2)}) collective-permute-start(f32[2,1,128,128]{3,2,1,0:T(8,128)S(1)} %get-tuple-element.198), channel_id=1, source_target_pairs={{1,0},{2,1},{3,2},{5,4},{6,5},{7,6},{9,8},{10,9},{11,10},{13,12},{... | collective-permute-start | bytes 393224 | tf_op jit(solution)/shard_map/ppermute | solution.py:27
  77.0 129.2 %copy-start.3 = (f32[4,256,256]{2,1,0:T(8,128)S(1)}, f32[4,256,256]{2,1,0:T(8,128)}, u32[]{:S(2)}) copy-start(f32[4,256,256]{2,1,0:T(8,128)} %all-reduce.2.cloned.1.call-done) | copy-start | bytes 3145732
  77.0 6.0 %collective-permute-start = (f32[2,128,128]{2,1,0:T(8,128)S(1)}, f32[2,128,128]{2,1,0:T(8,128)S(1)}, u32[]{:S(2)}, u32[]{:S(2)}) collective-permute-start(f32[2,128,128]{2,1,0:T(8,128)S(1)} %get-tuple-element.307), channel_id=1, source_target_pairs={{0,1},{1,2},{2,3},{4,5},{5,6},{6,7},{8,9},{9,10},{10,11},{12,13},{... | collective-permute-start | bytes 393224 | tf_op jit(solution)/shard_map/while/body/eval_jaxpr/ppermute | solution.py:26
  80.5 6.9 %collective-permute-start.1 = (f32[2,128,128]{2,1,0:T(8,128)S(1)}, f32[2,128,128]{2,1,0:T(8,128)S(1)}, u32[]{:S(2)}, u32[]{:S(2)}) collective-permute-start(f32[2,128,128]{2,1,0:T(8,128)S(1)} %get-tuple-element.307), channel_id=1, source_target_pairs={{1,0},{2,1},{3,2},{5,4},{6,5},{7,6},{9,8},{10,9},{11,10},{13,12},{... | collective-permute-start | bytes 393224 | tf_op jit(solution)/shard_map/while/body/eval_jaxpr/ppermute | solution.py:27
  88.6 6.3 %collective-permute-start.2 = (f32[2,128,128]{2,1,0:T(8,128)S(1)}, f32[2,128,128]{2,1,0:T(8,128)S(1)}, u32[]{:S(2)}, u32[]{:S(2)}) collective-permute-start(f32[2,128,128]{2,1,0:T(8,128)S(1)} %fusion.173), channel_id=1, source_target_pairs={{0,4},{4,8},{8,12},{12,16},{16,20},{20,24},{24,28},{1,5},{5,9},{9,... | collective-permute-start | bytes 393224 | tf_op jit(solution)/shard_map/while/body/eval_jaxpr/ppermute | solution.py:35
  94.9 5.9 %collective-permute-start = (f32[2,128,128]{2,1,0:T(8,128)S(1)}, f32[2,128,128]{2,1,0:T(8,128)S(1)}, u32[]{:S(2)}, u32[]{:S(2)}) collective-permute-start(f32[2,128,128]{2,1,0:T(8,128)S(1)} %get-tuple-element.307), channel_id=1, source_target_pairs={{0,1},{1,2},{2,3},{4,5},{5,6},{6,7},{8,9},{9,10},{10,11},{12,13},{... | collective-permute-start | bytes 393224 | tf_op jit(solution)/shard_map/while/body/eval_jaxpr/ppermute | solution.py:26
  98.3 6.9 %collective-permute-start.1 = (f32[2,128,128]{2,1,0:T(8,128)S(1)}, f32[2,128,128]{2,1,0:T(8,128)S(1)}, u32[]{:S(2)}, u32[]{:S(2)}) collective-permute-start(f32[2,128,128]{2,1,0:T(8,128)S(1)} %get-tuple-element.307), channel_id=1, source_target_pairs={{1,0},{2,1},{3,2},{5,4},{6,5},{7,6},{9,8},{10,9},{11,10},{13,12},{... | collective-permute-start | bytes 393224 | tf_op jit(solution)/shard_map/while/body/eval_jaxpr/ppermute | solution.py:27
  106.4 6.3 %collective-permute-start.2 = (f32[2,128,128]{2,1,0:T(8,128)S(1)}, f32[2,128,128]{2,1,0:T(8,128)S(1)}, u32[]{:S(2)}, u32[]{:S(2)}) collective-permute-start(f32[2,128,128]{2,1,0:T(8,128)S(1)} %fusion.173), channel_id=1, source_target_pairs={{0,4},{4,8},{8,12},{12,16},{16,20},{20,24},{24,28},{1,5},{5,9},{9,... | collective-permute-start | bytes 393224 | tf_op jit(solution)/shard_map/while/body/eval_jaxpr/ppermute | solution.py:35
  112.7 6.3 %collective-permute-start = (f32[2,128,128]{2,1,0:T(8,128)S(1)}, f32[2,128,128]{2,1,0:T(8,128)S(1)}, u32[]{:S(2)}, u32[]{:S(2)}) collective-permute-start(f32[2,128,128]{2,1,0:T(8,128)S(1)} %get-tuple-element.307), channel_id=1, source_target_pairs={{0,1},{1,2},{2,3},{4,5},{5,6},{6,7},{8,9},{9,10},{10,11},{12,13},{... | collective-permute-start | bytes 393224 | tf_op jit(solution)/shard_map/while/body/eval_jaxpr/ppermute | solution.py:26
  116.1 7.0 %collective-permute-start.1 = (f32[2,128,128]{2,1,0:T(8,128)S(1)}, f32[2,128,128]{2,1,0:T(8,128)S(1)}, u32[]{:S(2)}, u32[]{:S(2)}) collective-permute-start(f32[2,128,128]{2,1,0:T(8,128)S(1)} %get-tuple-element.307), channel_id=1, source_target_pairs={{1,0},{2,1},{3,2},{5,4},{6,5},{7,6},{9,8},{10,9},{11,10},{13,12},{... | collective-permute-start | bytes 393224 | tf_op jit(solution)/shard_map/while/body/eval_jaxpr/ppermute | solution.py:27
  124.4 6.3 %collective-permute-start.2 = (f32[2,128,128]{2,1,0:T(8,128)S(1)}, f32[2,128,128]{2,1,0:T(8,128)S(1)}, u32[]{:S(2)}, u32[]{:S(2)}) collective-permute-start(f32[2,128,128]{2,1,0:T(8,128)S(1)} %fusion.173), channel_id=1, source_target_pairs={{0,4},{4,8},{8,12},{12,16},{16,20},{20,24},{24,28},{1,5},{5,9},{9,... | collective-permute-start | bytes 393224 | tf_op jit(solution)/shard_map/while/body/eval_jaxpr/ppermute | solution.py:35
  130.7 5.6 %collective-permute-start = (f32[2,128,128]{2,1,0:T(8,128)S(1)}, f32[2,128,128]{2,1,0:T(8,128)S(1)}, u32[]{:S(2)}, u32[]{:S(2)}) collective-permute-start(f32[2,128,128]{2,1,0:T(8,128)S(1)} %get-tuple-element.307), channel_id=1, source_target_pairs={{0,1},{1,2},{2,3},{4,5},{5,6},{6,7},{8,9},{9,10},{10,11},{12,13},{... | collective-permute-start | bytes 393224 | tf_op jit(solution)/shard_map/while/body/eval_jaxpr/ppermute | solution.py:26
  132.9 7.5 %collective-permute-start.1 = (f32[2,128,128]{2,1,0:T(8,128)S(1)}, f32[2,128,128]{2,1,0:T(8,128)S(1)}, u32[]{:S(2)}, u32[]{:S(2)}) collective-permute-start(f32[2,128,128]{2,1,0:T(8,128)S(1)} %get-tuple-element.307), channel_id=1, source_target_pairs={{1,0},{2,1},{3,2},{5,4},{6,5},{7,6},{9,8},{10,9},{11,10},{13,12},{... | collective-permute-start | bytes 393224 | tf_op jit(solution)/shard_map/while/body/eval_jaxpr/ppermute | solution.py:27
  141.6 6.3 %collective-permute-start.2 = (f32[2,128,128]{2,1,0:T(8,128)S(1)}, f32[2,128,128]{2,1,0:T(8,128)S(1)}, u32[]{:S(2)}, u32[]{:S(2)}) collective-permute-start(f32[2,128,128]{2,1,0:T(8,128)S(1)} %fusion.173), channel_id=1, source_target_pairs={{0,4},{4,8},{8,12},{12,16},{16,20},{20,24},{24,28},{1,5},{5,9},{9,... | collective-permute-start | bytes 393224 | tf_op jit(solution)/shard_map/while/body/eval_jaxpr/ppermute | solution.py:35
  147.9 5.6 %collective-permute-start = (f32[2,128,128]{2,1,0:T(8,128)S(1)}, f32[2,128,128]{2,1,0:T(8,128)S(1)}, u32[]{:S(2)}, u32[]{:S(2)}) collective-permute-start(f32[2,128,128]{2,1,0:T(8,128)S(1)} %get-tuple-element.307), channel_id=1, source_target_pairs={{0,1},{1,2},{2,3},{4,5},{5,6},{6,7},{8,9},{9,10},{10,11},{12,13},{... | collective-permute-start | bytes 393224 | tf_op jit(solution)/shard_map/while/body/eval_jaxpr/ppermute | solution.py:26
  150.1 7.5 %collective-permute-start.1 = (f32[2,128,128]{2,1,0:T(8,128)S(1)}, f32[2,128,128]{2,1,0:T(8,128)S(1)}, u32[]{:S(2)}, u32[]{:S(2)}) collective-permute-start(f32[2,128,128]{2,1,0:T(8,128)S(1)} %get-tuple-element.307), channel_id=1, source_target_pairs={{1,0},{2,1},{3,2},{5,4},{6,5},{7,6},{9,8},{10,9},{11,10},{13,12},{... | collective-permute-start | bytes 393224 | tf_op jit(solution)/shard_map/while/body/eval_jaxpr/ppermute | solution.py:27
  158.8 6.3 %collective-permute-start.2 = (f32[2,128,128]{2,1,0:T(8,128)S(1)}, f32[2,128,128]{2,1,0:T(8,128)S(1)}, u32[]{:S(2)}, u32[]{:S(2)}) collective-permute-start(f32[2,128,128]{2,1,0:T(8,128)S(1)} %fusion.173), channel_id=1, source_target_pairs={{0,4},{4,8},{8,12},{12,16},{16,20},{20,24},{24,28},{1,5},{5,9},{9,... | collective-permute-start | bytes 393224 | tf_op jit(solution)/shard_map/while/body/eval_jaxpr/ppermute | solution.py:35
  165.1 5.6 %collective-permute-start = (f32[2,128,128]{2,1,0:T(8,128)S(1)}, f32[2,128,128]{2,1,0:T(8,128)S(1)}, u32[]{:S(2)}, u32[]{:S(2)}) collective-permute-start(f32[2,128,128]{2,1,0:T(8,128)S(1)} %get-tuple-element.307), channel_id=1, source_target_pairs={{0,1},{1,2},{2,3},{4,5},{5,6},{6,7},{8,9},{9,10},{10,11},{12,13},{... | collective-permute-start | bytes 393224 | tf_op jit(solution)/shard_map/while/body/eval_jaxpr/ppermute | solution.py:26
  167.3 7.5 %collective-permute-start.1 = (f32[2,128,128]{2,1,0:T(8,128)S(1)}, f32[2,128,128]{2,1,0:T(8,128)S(1)}, u32[]{:S(2)}, u32[]{:S(2)}) collective-permute-start(f32[2,128,128]{2,1,0:T(8,128)S(1)} %get-tuple-element.307), channel_id=1, source_target_pairs={{1,0},{2,1},{3,2},{5,4},{6,5},{7,6},{9,8},{10,9},{11,10},{13,12},{... | collective-permute-start | bytes 393224 | tf_op jit(solution)/shard_map/while/body/eval_jaxpr/ppermute | solution.py:27
  176.0 6.3 %collective-permute-start.2 = (f32[2,128,128]{2,1,0:T(8,128)S(1)}, f32[2,128,128]{2,1,0:T(8,128)S(1)}, u32[]{:S(2)}, u32[]{:S(2)}) collective-permute-start(f32[2,128,128]{2,1,0:T(8,128)S(1)} %fusion.173), channel_id=1, source_target_pairs={{0,4},{4,8},{8,12},{12,16},{16,20},{20,24},{24,28},{1,5},{5,9},{9,... | collective-permute-start | bytes 393224 | tf_op jit(solution)/shard_map/while/body/eval_jaxpr/ppermute | solution.py:35
  182.3 5.6 %collective-permute-start = (f32[2,128,128]{2,1,0:T(8,128)S(1)}, f32[2,128,128]{2,1,0:T(8,128)S(1)}, u32[]{:S(2)}, u32[]{:S(2)}) collective-permute-start(f32[2,128,128]{2,1,0:T(8,128)S(1)} %get-tuple-element.307), channel_id=1, source_target_pairs={{0,1},{1,2},{2,3},{4,5},{5,6},{6,7},{8,9},{9,10},{10,11},{12,13},{... | collective-permute-start | bytes 393224 | tf_op jit(solution)/shard_map/while/body/eval_jaxpr/ppermute | solution.py:26
  184.5 7.5 %collective-permute-start.1 = (f32[2,128,128]{2,1,0:T(8,128)S(1)}, f32[2,128,128]{2,1,0:T(8,128)S(1)}, u32[]{:S(2)}, u32[]{:S(2)}) collective-permute-start(f32[2,128,128]{2,1,0:T(8,128)S(1)} %get-tuple-element.307), channel_id=1, source_target_pairs={{1,0},{2,1},{3,2},{5,4},{6,5},{7,6},{9,8},{10,9},{11,10},{13,12},{... | collective-permute-start | bytes 393224 | tf_op jit(solution)/shard_map/while/body/eval_jaxpr/ppermute | solution.py:27
  193.2 6.3 %collective-permute-start.2 = (f32[2,128,128]{2,1,0:T(8,128)S(1)}, f32[2,128,128]{2,1,0:T(8,128)S(1)}, u32[]{:S(2)}, u32[]{:S(2)}) collective-permute-start(f32[2,128,128]{2,1,0:T(8,128)S(1)} %fusion.173), channel_id=1, source_target_pairs={{0,4},{4,8},{8,12},{12,16},{16,20},{20,24},{24,28},{1,5},{5,9},{9,... | collective-permute-start | bytes 393224 | tf_op jit(solution)/shard_map/while/body/eval_jaxpr/ppermute | solution.py:35
  199.9 9.3 %collective-permute-start.6 = (f32[2,128,128]{2,1,0:T(8,128)S(1)}, f32[2,128,128]{2,1,0:T(8,128)S(1)}, u32[]{:S(2)}, u32[]{:S(2)}) collective-permute-start(f32[2,128,128]{2,1,0:T(8,128)S(1)} %get-tuple-element.121), channel_id=1, source_target_pairs={{1,0},{2,1},{3,2},{5,4},{6,5},{7,6},{9,8},{10,9},{11,10},{13,12},{... | collective-permute-start | bytes 393224 | tf_op jit(solution)/shard_map/ppermute | solution.py:27
  201.2 7.9 %collective-permute-start.5 = (f32[2,128,128]{2,1,0:T(8,128)S(1)}, f32[2,128,128]{2,1,0:T(8,128)S(1)}, u32[]{:S(2)}, u32[]{:S(2)}) collective-permute-start(f32[2,128,128]{2,1,0:T(8,128)S(1)} %get-tuple-element.121), channel_id=1, source_target_pairs={{0,1},{1,2},{2,3},{4,5},{5,6},{6,7},{8,9},{9,10},{10,11},{12,13},{... | collective-permute-start | bytes 393224 | tf_op jit(solution)/shard_map/ppermute | solution.py:26
  209.5 0.9 copy-start.8
  209.6 1.6 copy-start.5
  213.5 21.0 %collective-permute-start.8 = (f32[3,1,256,256]{3,2,1,0:T(8,128)S(1)}, f32[3,1,256,256]{3,2,1,0:T(8,128)S(1)}, u32[]{:S(2)}, u32[]{:S(2)}) collective-permute-start(f32[3,1,256,256]{3,2,1,0:T(8,128)S(1)} %get-tuple-element.159), channel_id=1, source_target_pairs={{0,1},{1,2},{2,3},{4,5},{5,6},{6,7},{8,9},{9,10},{10,11},{12,13},{... | collective-permute-start | bytes 2359304 | tf_op jit(solution)/shard_map/ppermute | solution.py:26
  217.9 20.7 %collective-permute-start.7 = (f32[3,1,256,256]{3,2,1,0:T(8,128)S(1)}, f32[3,1,256,256]{3,2,1,0:T(8,128)S(1)}, u32[]{:S(2)}, u32[]{:S(2)}) collective-permute-start(f32[3,1,256,256]{3,2,1,0:T(8,128)S(1)} %get-tuple-element.160), channel_id=1, source_target_pairs={{1,0},{2,1},{3,2},{5,4},{6,5},{7,6},{9,8},{10,9},{11,10},{13,12},{... | collective-permute-start | bytes 2359304 | tf_op jit(solution)/shard_map/ppermute | solution.py:27
  221.1 18.4 %copy-start.1 = (f32[4,256,256]{2,1,0:T(8,128)S(1)}, f32[4,256,256]{2,1,0:T(8,128)}, u32[]{:S(2)}) copy-start(f32[4,256,256]{2,1,0:T(8,128)} %param.7) | copy-start | bytes 3145732
  221.1 18.4 %copy-start.2 = (f32[1,4,256,256]{3,2,1,0:T(8,128)S(1)}, f32[1,4,256,256]{3,2,1,0:T(8,128)}, u32[]{:S(2)}) copy-start(f32[1,4,256,256]{3,2,1,0:T(8,128)} %param.6) | copy-start | bytes 3145732
  234.4 4.2 %copy-start.6 = (f32[3,1,256,256]{3,2,1,0:T(8,128)}, f32[3,1,256,256]{3,2,1,0:T(8,128)S(1)}, u32[]{:S(2)}) copy-start(f32[3,1,256,256]{3,2,1,0:T(8,128)S(1)} %collective-permute-done.8) | copy-start | bytes 2359300
  238.6 0.9 copy-start.7
  246.4 6.4 %collective-permute-start.10 = (f32[1,256,256]{2,1,0:T(8,128)S(1)}, f32[1,256,256]{2,1,0:T(8,128)S(1)}, u32[]{:S(2)}, u32[]{:S(2)}) collective-permute-start(f32[1,256,256]{2,1,0:T(8,128)S(1)} %get-tuple-element.169), channel_id=1, source_target_pairs={{0,1},{1,2},{2,3},{4,5},{5,6},{6,7},{8,9},{9,10},{10,11},{12,13},{... | collective-permute-start | bytes 786440 | tf_op jit(solution)/shard_map/ppermute | solution.py:26
  248.6 8.3 %collective-permute-start.9 = (f32[1,256,256]{2,1,0:T(8,128)S(1)}, f32[1,256,256]{2,1,0:T(8,128)S(1)}, u32[]{:S(2)}, u32[]{:S(2)}) collective-permute-start(f32[1,256,256]{2,1,0:T(8,128)S(1)} %get-tuple-element.170), channel_id=1, source_target_pairs={{1,0},{2,1},{3,2},{5,4},{6,5},{7,6},{9,8},{10,9},{11,10},{13,12},{... | collective-permute-start | bytes 786440 | tf_op jit(solution)/shard_map/ppermute | solution.py:27
Sparse Core Ops, SparseCore 0:
  16.8 58.0 all-reduce.1
where the time goes:
time: 268 us; the launch traced here: 267 us
  waiting for transfers between devices  154 us (57%)
  starting transfers between devices  61.6 us (23%)
  other arithmetic  16.3 us (6%)
  between operations  13.9 us (5%)
  local copies, waits for them, and re-layouts  10.2 us (4%)
  matrix products  9.94 us (4%)
    psum x1, waiting for transfers between devices, broadcast(): return lax.psum(jnp.where(mine, array, jnp.zeros_like(array)), axis)  53.8 us
    ppermute x11, waiting for transfers between devices, padded_2(): after = lax.ppermute(first, axis, down)  40.2 us
    ppermute x11, starting transfers between devices, padded_2(): before = lax.ppermute(last, axis, up)  33.8 us
    ppermute x7, waiting for transfers between devices, shifted(): lax.ppermute(value, axis, [(source, source + steps) for source in range(f...  30.5 us
    ppermute x11, waiting for transfers between devices, padded_2(): before = lax.ppermute(last, axis, up)  29.9 us
    ppermute x11, starting transfers between devices, padded_2(): after = lax.ppermute(first, axis, down)  14.4 us
    ppermute x7, starting transfers between devices, shifted(): lax.ppermute(value, axis, [(source, source + steps) for source in range(f...  13.4 us
    slice x36, local copies, waits for them, and re-layouts, tendency(): plus_y = jnp.roll(middle, -1, axis=-1)  6.88 us
  transfers between devices with their start and end apart: 30, of which 28 were waited for; matrix products, arithmetic and copies ran while one was open for 2% of the time, Pallas kernels for 0%

commit v1 on v0

v1 whole, which is shorter than its diff:
```python
import functools

import jax
import jax.numpy as jnp
from jax import lax
from jax.experimental import pallas as pl
from jax.experimental.pallas import tpu as pltpu
from jax.sharding import PartitionSpec as P

diffusion = 0.1
speed_z = 0.4
speed_x = 0.3
speed_y = 0.2
weights_one = (5.0 / 24.0, 1.0 / 3.0, -1.0 / 24.0)
weights_two = (-1.0 / 24.0, 1.0 / 3.0, 5.0 / 24.0)


def tendency(padded, rate_field, source_term, spacing):
    middle = padded[..., 1:-1, :, :]
    upper_z = padded[..., 2:, :, :]
    lower_z = padded[..., :-2, :, :]
    plus_x = jnp.roll(middle, -1, axis=-2)
    minus_x = jnp.roll(middle, 1, axis=-2)
    plus_y = jnp.roll(middle, -1, axis=-1)
    minus_y = jnp.roll(middle, 1, axis=-1)
    laplacian = (upper_z + lower_z + plus_x + minus_x + plus_y + minus_y - 6.0 * middle) / (
        spacing * spacing
    )
    transport = (
        speed_z * (upper_z - lower_z) + speed_x * (plus_x - minus_x) + speed_y * (plus_y - minus_y)
    ) / (2.0 * spacing)
    return (
        diffusion * laplacian
        - transport
        + rate_field * middle / (1.0 + middle * middle)
        + source_term
    )


def pair_table(count):
    fine_index = jnp.arange(count, dtype=jnp.int32)[:, None]
    coarse_index = jnp.arange(count // 2, dtype=jnp.int32)[None, :]
    return (fine_index // 2 == coarse_index).astype(jnp.float32)


def restrict(field):
    count_z, count_x, count_y = field.shape[-3:]
    paired = field.reshape(field.shape[:-3] + (count_z // 2, 2, count_x, count_y))
    summed_z = paired[..., 0, :, :] + paired[..., 1, :, :]
    summed_y = jnp.einsum(
        "...xy,yb->...xb", summed_z, pair_table(count_y), precision=lax.Precision.HIGHEST
    )
    summed_x = jnp.einsum(
        "...xb,xa->...ab", summed_y, pair_table(count_x), precision=lax.Precision.HIGHEST
    )
    return 0.125 * summed_x


def inject(coarse):
    count_x, count_y = coarse.shape[-2:]
    along_y = jnp.einsum(
        "...ab,yb->...ay", coarse, pair_table(2 * count_y), precision=lax.Precision.HIGHEST
    )
    along_x = jnp.einsum(
        "...ay,xa->...xy", along_y, pair_table(2 * count_x), precision=lax.Precision.HIGHEST
    )
    return along_x


MESH = pl.DeviceIdType.MESH


def coarse_tendency(middle, upper_z, lower_z, rate_field, source_term):
    flow = diffusion / 4.0
    drift_z, drift_x, drift_y = speed_z / 4.0, speed_x / 4.0, speed_y / 4.0
    count_x, count_y = middle.shape
    plus_x = pltpu.roll(middle, count_x - 1, 0)
    minus_x = pltpu.roll(middle, 1, 0)
    plus_y = pltpu.roll(middle, count_y - 1, 1)
    minus_y = pltpu.roll(middle, 1, 1)
    return (
        (flow - drift_z) * upper_z
        + (flow + drift_z) * lower_z
        + (flow - drift_x) * plus_x
        + (flow + drift_x) * minus_x
        + (flow - drift_y) * plus_y
        + (flow + drift_y) * minus_y
        - 6.0 * flow * middle
        + rate_field * middle / (1.0 + middle * middle)
        + source_term
    )


def chain_kernel(
    count_t, count_s, detail, warm_c, rate_c, source_c,
    seed_detail, halo, start_out, first_out, second_out,
    start, rate_wide, source_wide, send_sem, recv_sem, seed_sem,
):
    rank, slab = lax.axis_index("tm"), lax.axis_index("space")
    last = count_t - 1
    layers, depth = warm_c.shape[0], detail.shape[0]
    above, below = slab < count_s - 1, slab > 0
    slab_up, slab_down = jnp.minimum(slab + 1, count_s - 1), jnp.maximum(slab - 1, 0)
    following = lax.rem(rank + 1, count_t)

    def copy(source, target, index, to_rank, to_slab):
        return pltpu.make_async_remote_copy(
            src_ref=source,
            dst_ref=target,
            send_sem=send_sem.at[index],
            recv_sem=recv_sem.at[index],
            device_id={"tm": to_rank, "space": to_slab},
            device_id_type=MESH,
        )

    def chain_copies(value):
        return (
            copy(value, start.at[0:layers], 6, following, slab_up),
            copy(value, start.at[layers : 2 * layers], 7, following, slab),
            copy(value, start.at[2 * layers : 3 * layers], 8, following, slab_down),
        )

    own_second = second_out.at[1 : layers + 1]
    chain_seed = chain_copies(warm_c)
    chain_next = chain_copies(own_second)
    ups = (
        copy(source_c.at[layers - 1 : layers], source_wide.at[0:1], 0, rank, slab_up),
        copy(rate_c.at[layers - 1 : layers], rate_wide.at[0:1], 1, rank, slab_up),
        copy(detail.at[depth - 1 : depth], halo.at[0:1], 2, rank, slab_up),
    )
    downs = (
        copy(source_c.at[0:1], source_wide.at[layers + 1 : layers + 2], 3, rank, slab_down),
        copy(rate_c.at[0:1], rate_wide.at[layers + 1 : layers + 2], 4, rank, slab_down),
        copy(detail.at[0:1], halo.at[1:2], 5, rank, slab_down),
    )
    edge_up = copy(second_out.at[layers : layers + 1], second_out.at[0:1], 9, rank, slab_up)
    edge_down = copy(second_out.at[1:2], second_out.at[layers + 1 : layers + 2], 10, rank, slab_down)

    targets = [last - 1] + list(range(last - 2, -1, -2))
    seeds, seed_halos = [], []
    for place, target in enumerate(targets):
        for kind, group, source, region in (
            (0, seeds, detail, seed_detail.at[0:depth]),
            (1, seed_halos, halo, seed_detail.at[depth : depth + 2]),
        ):
            group.append(
                pltpu.make_async_remote_copy(
                    src_ref=source,
                    dst_ref=region,
                    send_sem=seed_sem.at[kind, place],
                    recv_sem=recv_sem.at[11 + kind],
                    device_id={"tm": target, "space": slab},
                    device_id_type=MESH,
                )
            )
    partner = jnp.maximum(rank - 1, 0)
    passed = (
        copy(seed_detail.at[0:depth], seed_detail.at[0:depth], 11, partner, slab),
        copy(seed_detail.at[depth : depth + 2], seed_detail.at[depth : depth + 2], 12, partner, slab),
    )
    is_last = rank == last
    leader = (rank < last) & (lax.rem(last - rank, 2) == 0)

    def each(condition, copies, act):
        @pl.when(condition)
        def _():
            for item in copies:
                getattr(item, act)()

    each(is_last & above, chain_seed[0:1], "start")
    each(is_last, chain_seed[1:2], "start")
    each(is_last & below, chain_seed[2:3], "start")
    each(above, ups, "start")
    each(below, downs, "start")
    each(is_last, seeds, "start")

    source_wide[1 : layers + 1] = source_c[...]
    rate_wide[1 : layers + 1] = rate_c[...]

    @pl.when(jnp.logical_not(below))
    def _():
        for ref in (source_wide, rate_wide, halo, second_out):
            ref[0:1] = jnp.zeros((1,) + ref.shape[1:], jnp.float32)
        start[0:layers] = jnp.zeros((layers,) + start.shape[1:], jnp.float32)

    @pl.when(jnp.logical_not(above))
    def _():
        for ref in (source_wide, rate_wide, halo, second_out):
            end = ref.shape[0]
            ref[end - 1 : end] = jnp.zeros((1,) + ref.shape[1:], jnp.float32)
        start[2 * layers : 3 * layers] = jnp.zeros((layers,) + start.shape[1:], jnp.float32)

    each(below, ups, "wait_recv")
    each(above, downs, "wait_recv")
    each(is_last, seed_halos, "start")

    @pl.when(is_last)
    def _():
        @pl.loop(0, depth)
        def _(layer):
            seed_detail[layer] = detail[layer]

        @pl.loop(0, 2)
        def _(side):
            seed_detail[depth + side] = halo[side]

    each(below, chain_seed[0:1], "wait_recv")
    each(rank >= 0, chain_seed[1:2], "wait_recv")
    each(above, chain_seed[2:3], "wait_recv")

    for layer in range(layers + 2):
        at = layer + layers - 1
        middle = start[at]
        value = middle + 0.5 * coarse_tendency(
            middle, start[at + 1], start[at - 1], rate_wide[layer], source_wide[layer]
        )
        if layer == 0:
            value = jnp.where(below, value, 0.0)
        if layer == layers + 1:
            value = jnp.where(above, value, 0.0)
        first_out[layer] = value
    for layer in range(1, layers + 1):
        middle = first_out[layer]
        second_out[layer] = middle + 0.5 * coarse_tendency(
            middle, first_out[layer + 1], first_out[layer - 1], rate_wide[layer], source_wide[layer]
        )

    going = rank < last
    each(going, chain_next[1:2], "start")
    each(going & above, chain_next[0:1], "start")
    each(going & below, chain_next[2:3], "start")
    each(above, (edge_up,), "start")
    each(below, (edge_down,), "start")
    start_out[...] = start[layers - 1 : 2 * layers + 1]

    each(going, passed, "wait_recv")
    each(leader, passed, "start")
    each(below, (edge_up,), "wait_recv")
    each(above, (edge_down,), "wait_recv")
    each(above, ups + (edge_up,) + chain_next[0:1], "wait_send")
    each(below, downs + (edge_down,) + chain_next[2:3], "wait_send")
    each(rank >= 0, chain_next[1:2], "wait_send")
    each(is_last, seeds + seed_halos, "wait_send")
    each(leader, passed, "wait_send")


def run_chain(mesh, detail, warm_c, rate_c, source_c):
    count_t, count_s = mesh.shape["tm"], mesh.shape["space"]
    layers, across, along = warm_c.shape
    depth, fine_x, fine_y = detail.shape
    wide = jax.ShapeDtypeStruct((layers + 2, across, along), jnp.float32)
    vmem = pl.BlockSpec(memory_space=pltpu.VMEM)
    return pl.pallas_call(
        functools.partial(chain_kernel, count_t, count_s),
        out_shape=[
            jax.ShapeDtypeStruct((depth + 2, fine_x, fine_y), jnp.float32),
            jax.ShapeDtypeStruct((2, fine_x, fine_y), jnp.float32),
            wide, wide, wide,
        ],
        in_specs=[vmem] * 4,
        out_specs=[vmem] * 5,
        scratch_shapes=[
            pltpu.VMEM((3 * layers, across, along), jnp.float32),
            pltpu.VMEM((layers + 2, across, along), jnp.float32),
            pltpu.VMEM((layers + 2, across, along), jnp.float32),
            pltpu.SemaphoreType.DMA((13,)),
            pltpu.SemaphoreType.DMA((13,)),
            pltpu.SemaphoreType.DMA((2, count_t // 2)),
        ],
        compiler_params=pltpu.CompilerParams(has_side_effects=True),
    )(detail, warm_c, rate_c, source_c)


def edge_kernel(count_s, value, halo, send_sem, recv_sem):
    rank, slab = lax.axis_index("tm"), lax.axis_index("space")
    depth = value.shape[0]
    above, below = slab < count_s - 1, slab > 0
    slab_up, slab_down = jnp.minimum(slab + 1, count_s - 1), jnp.maximum(slab - 1, 0)
    barrier = pltpu.get_barrier_semaphore()

    def copy(source, target, index, to_slab):
        return pltpu.make_async_remote_copy(
            src_ref=source,
            dst_ref=target,
            send_sem=send_sem.at[index],
            recv_sem=recv_sem.at[index],
            device_id={"tm": rank, "space": to_slab},
            device_id_type=MESH,
        )

    up = copy(value.at[depth - 1 : depth], halo.at[0:1], 0, slab_up)
    down = copy(value.at[0:1], halo.at[1:2], 1, slab_down)
    for there, to_slab in ((above, slab_up), (below, slab_down)):
        @pl.when(there)
        def _():
            pl.semaphore_signal(
                barrier, inc=1, device_id={"tm": rank, "space": to_slab}, device_id_type=MESH
            )

    @pl.when(above & below)
    def _():
        pl.semaphore_wait(barrier, 2)

    @pl.when(above != below)
    def _():
        pl.semaphore_wait(barrier, 1)

    @pl.when(above)
    def _():
        up.start()

    @pl.when(below)
    def _():
        down.start()

    @pl.when(jnp.logical_not(below))
    def _():
        halo[0:1] = jnp.zeros((1,) + halo.shape[1:], jnp.float32)

    @pl.when(jnp.logical_not(above))
    def _():
        halo[1:2] = jnp.zeros((1,) + halo.shape[1:], jnp.float32)

    @pl.when(below)
    def _():
        up.wait_recv()
        down.wait_send()

    @pl.when(above)
    def _():
        down.wait_recv()
        up.wait_send()


def exchange_edges(mesh, value):
    vmem = pl.BlockSpec(memory_space=pltpu.VMEM)
    return pl.pallas_call(
        functools.partial(edge_kernel, mesh.shape["space"]),
        out_shape=jax.ShapeDtypeStruct((2,) + value.shape[1:], jnp.float32),
        in_specs=[vmem],
        out_specs=vmem,
        scratch_shapes=[pltpu.SemaphoreType.DMA((2,)), pltpu.SemaphoreType.DMA((2,))],
        compiler_params=pltpu.CompilerParams(collective_id=1, has_side_effects=True),
    )(value)


def wrap(value, halo):
    return jnp.concatenate([halo[0:1], value, halo[1:2]], axis=0)


def spread(wide):
    layers = wide.shape[0] - 2
    fine = jnp.repeat(inject(wide), 2, axis=0)
    return fine[1 : 2 * layers + 3]


def shards(mesh, previous_end, source, rate):
    warm = previous_end[0]
    own_source = source[0]
    depth = warm.shape[0]
    warm_c = restrict(warm)
    rate_c = restrict(rate)
    source_c = restrict(own_source)
    detail = warm - jnp.repeat(inject(warm_c), 2, axis=0)
    seed_detail, halo, start, first, second = run_chain(mesh, detail, warm_c, rate_c, source_c)
    wide_detail = wrap(detail, halo)
    wide_seed = wrap(seed_detail[:depth], seed_detail[depth:])
    guess0 = wide_seed + spread(start)
    guess1 = wide_detail + spread(first)
    guess2 = wide_detail + spread(second)
    image0 = tendency(guess0, rate, own_source, 1.0)
    image1 = tendency(guess1, rate, own_source, 1.0)
    image2 = tendency(guess2, rate, own_source, 1.0)
    node_one = guess0[1:-1] + (
        weights_one[0] * image0 + weights_one[1] * image1 + weights_one[2] * image2
    )
    padded_one = wrap(node_one, exchange_edges(mesh, node_one))
    again = tendency(padded_one, rate, own_source, 1.0)
    node_two = (
        node_one
        + 0.5 * (again - image1)
        + (weights_two[0] * image0 + weights_two[1] * image1 + weights_two[2] * image2)
    )
    return jnp.stack([node_one, node_two])[None]


def solution(mesh):
    placed = (P("tm", "space", None, None), P("tm", "space", None, None), P("space", None, None))
    return jax.shard_map(
        functools.partial(shards, mesh),
        mesh=mesh,
        in_specs=placed,
        out_specs=P("tm", None, "space", None, None),
        check_vma=False,
    )
```

time: 268 us -> 104 us (0.39)
  the two profiles are of different devices: /device:TPU:2 before, /device:TPU:7 now
where the time goes in v1:
time: 104 us; the launch traced here: 103 us
  Pallas kernels  68.4 us (66%)
  local copies, waits for them, and re-layouts  11.8 us (11%)
  other arithmetic  11.7 us (11%)
  matrix products  11.1 us (11%)
    pallas_call x1, Pallas kernels, run_chain(): pl.pallas_call(functools.partial(chain_kernel, count_t, count_s), out_sha...  59.1 us
    pallas_call x1, Pallas kernels, exchange_edges(): pl.pallas_call(functools.partial(edge_kernel, mesh.shape['space']), out_s...  9.33 us
    unnamed x32, local copies, waits for them, and re-layouts  7.01 us
    add x1, other arithmetic, shards(): guess0[1:-1]  6.38 us
    dot_general x3, matrix products, restrict(): jnp.einsum('...xy,yb->...xb', summed_z, pair_table(count_y), precision=la...  3.83 us
    dot_general x4, matrix products, inject(): jnp.einsum('...ab,yb->...ay', coarse, pair_table(2 * count_y), precision=...  2.69 us
    dot_general x3, matrix products, restrict(): jnp.einsum('...xb,xa->...ab', summed_y, pair_table(count_x), precision=la...  2.37 us
    dot_general x4, matrix products, inject(): jnp.einsum('...ay,xa->...xy', along_y, pair_table(2 * count_x), precision...  2.26 us

profile of v1, /device:TPU:7, one launch (start us, length us, event | category | flops | bytes accessed | tf_op | source)
XLA Modules:
  0.0 103.4 jit_solution(1493860059972485208)
XLA Ops:
  0.0 1.7 %fusion.9 = f32[2,256,128]{2,1,0:T(8,128)S(1)} fusion(f32[2,2,256,256]{3,2,1,0:T(8,128)} %bitcast.90, s32[256]{0:T(256)S(1)} %and_select_fusion), kind=kOutput, calls=%fused_computation.47 | convolution fusion | flops 201490432 | bytes 1311744 | tf_op jit(solution)/shard_map/...xy,yb->...xb/dot_general | solution.py:50
  1.7 1.0 fusion.source_c
  2.8 1.6 %fusion.13 = f32[2,256,128]{2,1,0:T(8,128)S(1)} fusion(f32[2,2,256,256]{3,2,1,0:T(8,128)} %bitcast.91, s32[256]{0:T(256)S(1)} %and_select_fusion), kind=kOutput, calls=%fused_computation.51 | convolution fusion | flops 201490432 | bytes 1311744 | tf_op jit(solution)/shard_map/...xy,yb->...xb/dot_general | solution.py:50
  4.4 1.0 fusion.1.rate_c
  5.4 0.4 fusion.17
  5.9 0.4 fusion.2.warm_c
  6.2 0.3 fusion.36
  6.6 0.4 convolution_bitcast_fusion.3
  7.0 1.1 %bitcast_subtract_fusion.detail = f32[4,256,256]{2,1,0:T(8,128)} fusion(f32[1,4,256,256]{3,2,1,0:T(8,128)S(1)} %copy-done.10, f32[2,256,256]{2,1,0:T(8,128)S(1)} %convolution_bitcast_fusion.3), kind=kLoop, calls=%fused_computation.42 | loop fusion | flops 262144 | bytes 2621440 | tf_op jit(solution)/shard_map/sub | solution.py:364
  8.1 59.1 %shard_map.37 = (f32[6,256,256]{2,1,0:T(8,128)}, f32[2,256,256]{2,1,0:T(8,128)}, f32[4,128,128]{2,1,0:T(8,128)}, f32[4,128,128]{2,1,0:T(8,128)}, f32[4,128,128]{2,1,0:T(8,128)}) custom-call(f32[4,256,256]{2,1,0:T(8,128)} %bitcast_subtract_fusion.detail, f32[2,128,128]{2,1,0:T(8,128)} %copy-done.12, f32[2,128,128]{2,1,0:T(8,128)} %fusion.1.rate_c, ...), custom_call_target="tpu_custom_call" | custom-call | tf_op jit(solution)/shard_map/pallas_call | solution.py:253
  67.2 1.4 %fusion.31 = f32[4,128,256]{2,1,0:T(8,128)S(1)} fusion(f32[4,128,128]{2,1,0:T(8,128)} %get-tuple-element.11, s32[256]{0:T(256)S(1)} %and_select_fusion), kind=kOutput, calls=%fused_computation.61 | convolution fusion | flops 201359360 | bytes 787456 | tf_op jit(solution)/shard_map/...ab,yb->...ay/dot_general | solution.py:61
  68.6 0.6 convolution_bitcast_fusion.2
  69.3 0.5 fusion.28
  69.7 0.6 convolution_bitcast_fusion.1
  70.4 0.5 fusion.25
  70.8 0.6 convolution_bitcast_fusion
  71.4 0.2 broadcast_in_dim.13
  71.6 0.2 broadcast_in_dim.12
  71.8 0.2 broadcast_in_dim.11
  72.0 1.2 %copy-done.11 = f32[6,256,256]{2,1,0:T(8,128)S(1)} copy-done((f32[6,256,256]{2,1,0:T(8,128)S(1)}, f32[6,256,256]{2,1,0:T(8,128)}, u32[]{:S(2)}) %copy-start.11) | copy-done | bytes 1572888
  73.4 1.1 %copy-done.2 = f32[4,256,256]{2,1,0:T(8,128)S(1)} copy-done((f32[4,256,256]{2,1,0:T(8,128)S(1)}, f32[4,256,256]{2,1,0:T(8,128)}, u32[]{:S(2)}) %copy-start.2) | copy-done | bytes 1048600
  74.6 0.3 slice_add_fusion
  74.9 0.2 slice_add_fusion.2
  75.2 0.2 fusion.60
  75.4 0.2 fusion.56
  75.6 0.2 fusion.64
  75.8 0.3 fusion.59
  76.3 0.4 fusion.55
  76.7 0.2 fusion.53
  76.9 0.4 fusion.63
  77.2 0.2 fusion.61
  77.4 1.0 copy-done.3
  78.4 0.3 copy-done.5
  78.8 6.4 %add_add_fusion = (f32[4,256,256]{2,1,0:T(8,128)S(1)}, f32[4,256,256]{2,1,0:T(8,128)}, f32[4,256,256]{2,1,0:T(8,128)}, f32[4,256,256]{2,1,0:T(8,128)}) fusion(f32[1,4,256,256]{3,2,1,0:T(8,128)S(1)} %copy-done.3, f32[4,256,256]{2,1,0:T(8,128)S(1)} %copy-done.5, f32[6,256,256]{2,1,0:T(8,128)S(1)} %slice_add_fusion.2, f32[6,256,256]{2,1,0:T(8,128)S(1)} %get-tuple-element.28, ...), kind=kLoop, calls=%fused_computation.43 | loop fusion | flops 23592960 | bytes 28311552 | tf_op jit(solution)/shard_map/add | solution.py:374
  85.2 1.0 copy-done
  86.1 9.3 %shard_map.38 = f32[2,256,256]{2,1,0:T(8,128)} custom-call(f32[4,256,256]{2,1,0:T(8,128)} %copy-done), custom_call_target="tpu_custom_call" | custom-call | tf_op jit(solution)/shard_map/pallas_call | solution.py:337
  95.5 1.2 %fusion.70 = (f32[1,256,256]{2,1,0:T(8,128)S(1)}, f32[1,256,256]{2,1,0:T(8,128)S(1)}) fusion(f32[2,256,256]{2,1,0:T(8,128)} %shard_map.38), kind=kLoop, calls=%fused_computation.98 | loop fusion | bytes 1048576 | tf_op jit(solution)/shard_map/slice | solution.py:348
  96.6 0.2 copy-done.1
  96.9 0.2 fusion.69
  97.1 0.4 fusion.68
  97.5 0.2 fusion.66
  97.7 0.6 copy-done.9
  98.3 0.4 copy-done.4
  98.7 0.3 copy-done.6
  99.0 0.3 copy-done.7
  99.4 0.3 copy-done.8
  99.7 2.1 %fusion.7 = f32[1,4,256,256]{3,2,1,0:T(8,128)S(1)} fusion(f32[4,256,256]{2,1,0:T(8,128)S(1)} %copy-done.1, f32[4,256,256]{2,1,0:T(8,128)S(1)} %copy-done.7, f32[1,4,256,256]{3,2,1,0:T(8,128)S(1)} %copy-done.4, f32[4,256,256]{2,1,0:T(8,128)S(1)} %copy-done.9, f32[4,256,256]{2,1,0:T(8,128)S(1)} %copy-done.6, f32[4,256,255]{2,1,0:T(8,128)S(1)} %get-tuple-element.52, ...), kind=kLoop, calls=%fused_computation.41 | loop fusion | flops 11796480 | bytes 13107200 | tf_op jit(solution)/shard_map/stack | solution.py:384
  101.8 1.6 %maximum_bitcast_fusion = f32[1,2,4,256,256]{4,3,2,1,0:T(8,128)} fusion(f32[1,4,256,256]{3,2,1,0:T(8,128)S(1)} %fusion.7, f32[1,4,256,256]{3,2,1,0:T(8,128)S(1)} %bitcast.89), kind=kLoop, calls=%fused_computation | loop fusion | flops 524288 | bytes 4194304 | tf_op jit(solution)/shard_map/broadcast_in_dim | solution.py:384
  (29 shorter events, 0.5 us)
Async XLA Ops:
  0.0 5.4 %copy-start.10 = (f32[1,4,256,256]{3,2,1,0:T(8,128)S(1)}, f32[1,4,256,256]{3,2,1,0:T(8,128)}, u32[]{:S(2)}) copy-start(f32[1,4,256,256]{3,2,1,0:T(8,128)} %param.3) | copy-start | bytes 3145732
  6.2 1.8 %copy-start.12 = (f32[2,128,128]{2,1,0:T(8,128)}, f32[2,128,128]{2,1,0:T(8,128)S(1)}, u32[]{:S(2)}) copy-start(f32[2,128,128]{2,1,0:T(8,128)S(1)} %fusion.2.warm_c) | copy-start | bytes 393220
  67.2 2.1 %copy-start.15 = (f32[4,128,128]{2,1,0:T(8,128)S(1)}, f32[4,128,128]{2,1,0:T(8,128)}, u32[]{:S(2)}) copy-start(f32[4,128,128]{2,1,0:T(8,128)} %get-tuple-element.13) | copy-start | bytes 786436
  69.2 1.1 %copy-start.14 = (f32[4,128,128]{2,1,0:T(8,128)S(1)}, f32[4,128,128]{2,1,0:T(8,128)}, u32[]{:S(2)}) copy-start(f32[4,128,128]{2,1,0:T(8,128)} %get-tuple-element.14) | copy-start | bytes 786436
  71.8 1.4 %copy-start.11 = (f32[6,256,256]{2,1,0:T(8,128)S(1)}, f32[6,256,256]{2,1,0:T(8,128)}, u32[]{:S(2)}) copy-start(f32[6,256,256]{2,1,0:T(8,128)} %get-tuple-element.10) | copy-start | bytes 4718596
  72.0 1.4 %copy-start.13 = (f32[2,256,256]{2,1,0:T(8,128)S(1)}, f32[2,256,256]{2,1,0:T(8,128)}, u32[]{:S(2)}) copy-start(f32[2,256,256]{2,1,0:T(8,128)} %get-tuple-element.12) | copy-start | bytes 1572868
  73.4 1.2 %copy-start.2 = (f32[4,256,256]{2,1,0:T(8,128)S(1)}, f32[4,256,256]{2,1,0:T(8,128)}, u32[]{:S(2)}) copy-start(f32[4,256,256]{2,1,0:T(8,128)} %bitcast_subtract_fusion.detail) | copy-start | bytes 3145732
  77.2 1.2 %copy-start.3 = (f32[1,4,256,256]{3,2,1,0:T(8,128)S(1)}, f32[1,4,256,256]{3,2,1,0:T(8,128)}, u32[]{:S(2)}) copy-start(f32[1,4,256,256]{3,2,1,0:T(8,128)} %param.4) | copy-start | bytes 3145732
  77.2 1.5 %copy-start.5 = (f32[4,256,256]{2,1,0:T(8,128)S(1)}, f32[4,256,256]{2,1,0:T(8,128)}, u32[]{:S(2)}) copy-start(f32[4,256,256]{2,1,0:T(8,128)} %param.5) | copy-start | bytes 3145732
  85.1 1.0 copy-start
  95.5 1.4 %copy-start.1 = (f32[4,256,256]{2,1,0:T(8,128)S(1)}, f32[4,256,256]{2,1,0:T(8,128)}, u32[]{:S(2)}) copy-start(f32[4,256,256]{2,1,0:T(8,128)} %copy-done) | copy-start | bytes 3145732
  97.1 1.2 %copy-start.9 = (f32[4,256,256]{2,1,0:T(8,128)S(1)}, f32[4,256,256]{2,1,0:T(8,128)}, u32[]{:S(2)}) copy-start(f32[4,256,256]{2,1,0:T(8,128)} %get-tuple-element.18) | copy-start | bytes 3145732
  97.4 1.3 %copy-start.4 = (f32[1,4,256,256]{3,2,1,0:T(8,128)S(1)}, f32[1,4,256,256]{3,2,1,0:T(8,128)}, u32[]{:S(2)}) copy-start(f32[1,4,256,256]{3,2,1,0:T(8,128)} %param.4) | copy-start | bytes 3145732
  97.4 1.6 %copy-start.6 = (f32[4,256,256]{2,1,0:T(8,128)S(1)}, f32[4,256,256]{2,1,0:T(8,128)}, u32[]{:S(2)}) copy-start(f32[4,256,256]{2,1,0:T(8,128)} %param.5) | copy-start | bytes 3145732
  97.5 1.9 %copy-start.7 = (f32[4,256,256]{2,1,0:T(8,128)S(1)}, f32[4,256,256]{2,1,0:T(8,128)}, u32[]{:S(2)}) copy-start(f32[4,256,256]{2,1,0:T(8,128)} %get-tuple-element.16) | copy-start | bytes 3145732
  97.5 2.2 %copy-start.8 = (f32[4,256,256]{2,1,0:T(8,128)S(1)}, f32[4,256,256]{2,1,0:T(8,128)}, u32[]{:S(2)}) copy-start(f32[4,256,256]{2,1,0:T(8,128)} %get-tuple-element.17) | copy-start | bytes 3145732

commit v2 on v1

--- a/solution.py
+++ b/solution.py
@@ -15,28 +15,6 @@
 weights_two = (-1.0 / 24.0, 1.0 / 3.0, 5.0 / 24.0)
 
 
-def tendency(padded, rate_field, source_term, spacing):
-    middle = padded[..., 1:-1, :, :]
-    upper_z = padded[..., 2:, :, :]
-    lower_z = padded[..., :-2, :, :]
-    plus_x = jnp.roll(middle, -1, axis=-2)
-    minus_x = jnp.roll(middle, 1, axis=-2)
-    plus_y = jnp.roll(middle, -1, axis=-1)
-    minus_y = jnp.roll(middle, 1, axis=-1)
-    laplacian = (upper_z + lower_z + plus_x + minus_x + plus_y + minus_y - 6.0 * middle) / (
-        spacing * spacing
-    )
-    transport = (
-        speed_z * (upper_z - lower_z) + speed_x * (plus_x - minus_x) + speed_y * (plus_y - minus_y)
-    ) / (2.0 * spacing)
-    return (
-        diffusion * laplacian
-        - transport
-        + rate_field * middle / (1.0 + middle * middle)
-        + source_term
-    )
-
-
 def pair_table(count):
     fine_index = jnp.arange(count, dtype=jnp.int32)[:, None]
     coarse_index = jnp.arange(count // 2, dtype=jnp.int32)[None, :]
@@ -70,9 +48,9 @@
 MESH = pl.DeviceIdType.MESH
 
 
-def coarse_tendency(middle, upper_z, lower_z, rate_field, source_term):
-    flow = diffusion / 4.0
-    drift_z, drift_x, drift_y = speed_z / 4.0, speed_x / 4.0, speed_y / 4.0
+def layer_tendency(middle, upper_z, lower_z, rate_field, source_term, spacing):
+    flow, twice = diffusion / (spacing * spacing), 2.0 * spacing
+    drift_z, drift_x, drift_y = speed_z / twice, speed_x / twice, speed_y / twice
     count_x, count_y = middle.shape
     plus_x = pltpu.roll(middle, count_x - 1, 0)
     minus_x = pltpu.roll(middle, 1, 0)
@@ -211,8 +189,8 @@
     for layer in range(layers + 2):
         at = layer + layers - 1
         middle = start[at]
-        value = middle + 0.5 * coarse_tendency(
-            middle, start[at + 1], start[at - 1], rate_wide[layer], source_wide[layer]
+        value = middle + 0.5 * layer_tendency(
+            middle, start[at + 1], start[at - 1], rate_wide[layer], source_wide[layer], 2.0
         )
         if layer == 0:
             value = jnp.where(below, value, 0.0)
@@ -221,8 +199,8 @@
         first_out[layer] = value
     for layer in range(1, layers + 1):
         middle = first_out[layer]
-        second_out[layer] = middle + 0.5 * coarse_tendency(
-            middle, first_out[layer + 1], first_out[layer - 1], rate_wide[layer], source_wide[layer]
+        second_out[layer] = middle + 0.5 * layer_tendency(
+            middle, first_out[layer + 1], first_out[layer - 1], rate_wide[layer], source_wide[layer], 2.0
         )
 
     going = rank < last
@@ -271,16 +249,19 @@
     )(detail, warm_c, rate_c, source_c)
 
 
-def edge_kernel(count_s, value, halo, send_sem, recv_sem):
+def sweep_kernel(
+    count_s, detail, halo, seed_detail, start, first, second, rate, source,
+    nodes, edges, send_sem, recv_sem,
+):
     rank, slab = lax.axis_index("tm"), lax.axis_index("space")
-    depth = value.shape[0]
+    depth = detail.shape[0]
     above, below = slab < count_s - 1, slab > 0
     slab_up, slab_down = jnp.minimum(slab + 1, count_s - 1), jnp.maximum(slab - 1, 0)
     barrier = pltpu.get_barrier_semaphore()
 
-    def copy(source, target, index, to_slab):
+    def copy(origin, target, index, to_slab):
         return pltpu.make_async_remote_copy(
-            src_ref=source,
+            src_ref=origin,
             dst_ref=target,
             send_sem=send_sem.at[index],
             recv_sem=recv_sem.at[index],
@@ -288,8 +269,8 @@
             device_id_type=MESH,
         )
 
-    up = copy(value.at[depth - 1 : depth], halo.at[0:1], 0, slab_up)
-    down = copy(value.at[0:1], halo.at[1:2], 1, slab_down)
+    up = copy(nodes.at[0, depth - 1], edges.at[0], 0, slab_up)
+    down = copy(nodes.at[0, 0], edges.at[1], 1, slab_down)
     for there, to_slab in ((above, slab_up), (below, slab_down)):
         @pl.when(there)
         def _():
@@ -297,6 +278,52 @@
                 barrier, inc=1, device_id={"tm": rank, "space": to_slab}, device_id_type=MESH
             )
 
+    def guess(ref, ends, shift, coarse, layer):
+        if layer < 0:
+            base = ends[shift]
+        elif layer == depth:
+            base = ends[shift + 1]
+        else:
+            base = ref[layer]
+        return base + coarse[layer // 2 + 1]
+
+    def node_one(layer):
+        own, images = None, []
+        for ref, ends, shift, coarse in (
+            (seed_detail, seed_detail, depth, start),
+            (detail, halo, 0, first),
+            (detail, halo, 0, second),
+        ):
+            middle = guess(ref, ends, shift, coarse, layer)
+            own = middle if own is None else own
+            images.append(
+                layer_tendency(
+                    middle,
+                    guess(ref, ends, shift, coarse, layer + 1),
+                    guess(ref, ends, shift, coarse, layer - 1),
+                    rate[layer], source[layer], 1.0,
+                )
+            )
+        value = own + (
+            weights_one[0] * images[0] + weights_one[1] * images[1] + weights_one[2] * images[2]
+        )
+        nodes[0, layer] = value
+        nodes[1, layer] = value + (
+            weights_two[0] * images[0]
+            + (weights_two[1] - 0.5) * images[1]
+            + weights_two[2] * images[2]
+        )
+
+    def node_two(layer):
+        upper = edges[1] if layer == depth - 1 else nodes[0, layer + 1]
+        lower = edges[0] if layer == 0 else nodes[0, layer - 1]
+        nodes[1, layer] += 0.5 * layer_tendency(
+            nodes[0, layer], upper, lower, rate[layer], source[layer], 1.0
+        )
+
+    node_one(0)
+    node_one(depth - 1)
+
     @pl.when(above & below)
     def _():
         pl.semaphore_wait(barrier, 2)
@@ -315,11 +342,16 @@
 
     @pl.when(jnp.logical_not(below))
     def _():
-        halo[0:1] = jnp.zeros((1,) + halo.shape[1:], jnp.float32)
+        edges[0] = jnp.zeros(edges.shape[1:], jnp.float32)
 
     @pl.when(jnp.logical_not(above))
     def _():
-        halo[1:2] = jnp.zeros((1,) + halo.shape[1:], jnp.float32)
+        edges[1] = jnp.zeros(edges.shape[1:], jnp.float32)
+
+    for layer in range(1, depth - 1):
+        node_one(layer)
+    for layer in range(1, depth - 1):
+        node_two(layer)
 
     @pl.when(below)
     def _():
@@ -331,57 +363,39 @@
         down.wait_recv()
         up.wait_send()
 
-
-def exchange_edges(mesh, value):
+    node_two(0)
+    node_two(depth - 1)
+
+
+def run_sweep(mesh, *operands):
     vmem = pl.BlockSpec(memory_space=pltpu.VMEM)
+    shape = operands[0].shape
     return pl.pallas_call(
-        functools.partial(edge_kernel, mesh.shape["space"]),
-        out_shape=jax.ShapeDtypeStruct((2,) + value.shape[1:], jnp.float32),
-        in_specs=[vmem],
+        functools.partial(sweep_kernel, mesh.shape["space"]),
+        out_shape=jax.ShapeDtypeStruct((2,) + shape, jnp.float32),
+        in_specs=[vmem] * len(operands),
         out_specs=vmem,
-        scratch_shapes=[pltpu.SemaphoreType.DMA((2,)), pltpu.SemaphoreType.DMA((2,))],
+        scratch_shapes=[
+            pltpu.VMEM((2,) + shape[1:], jnp.float32),
+            pltpu.SemaphoreType.DMA((2,)),
+            pltpu.SemaphoreType.DMA((2,)),
+        ],
         compiler_params=pltpu.CompilerParams(collective_id=1, has_side_effects=True),
-    )(value)
-
-
-def wrap(value, halo):
-    return jnp.concatenate([halo[0:1], value, halo[1:2]], axis=0)
-
-
-def spread(wide):
-    layers = wide.shape[0] - 2
-    fine = jnp.repeat(inject(wide), 2, axis=0)
-    return fine[1 : 2 * layers + 3]
+    )(*operands)
 
 
 def shards(mesh, previous_end, source, rate):
     warm = previous_end[0]
     own_source = source[0]
-    depth = warm.shape[0]
     warm_c = restrict(warm)
     rate_c = restrict(rate)
     source_c = restrict(own_source)
     detail = warm - jnp.repeat(inject(warm_c), 2, axis=0)
     seed_detail, halo, start, first, second = run_chain(mesh, detail, warm_c, rate_c, source_c)
-    wide_detail = wrap(detail, halo)
-    wide_seed = wrap(seed_detail[:depth], seed_detail[depth:])
-    guess0 = wide_seed + spread(start)
-    guess1 = wide_detail + spread(first)
-    guess2 = wide_detail + spread(second)
-    image0 = tendency(guess0, rate, own_source, 1.0)
-    image1 = tendency(guess1, rate, own_source, 1.0)
-    image2 = tendency(guess2, rate, own_source, 1.0)
-    node_one = guess0[1:-1] + (
-        weights_one[0] * image0 + weights_one[1] * image1 + weights_one[2] * image2
-    )
-    padded_one = wrap(node_one, exchange_edges(mesh, node_one))
-    again = tendency(padded_one, rate, own_source, 1.0)
-    node_two = (
-        node_one
-        + 0.5 * (again - image1)
-        + (weights_two[0] * image0 + weights_two[1] * image1 + weights_two[2] * image2)
-    )
-    return jnp.stack([node_one, node_two])[None]
+    return run_sweep(
+        mesh, detail, halo, seed_detail,
+        inject(start), inject(first), inject(second), rate, own_source,
+    )[None]
 
 
 def solution(mesh):

time: 104 us -> 90.9 us (0.87)
  other arithmetic: 11.7 us -> 1.08 us
  local copies, waits for them, and re-layouts: 11.8 us -> 3.06 us
  Pallas kernels: 68.4 us -> 72.3 us
  matrix products: 11.1 us -> 14.2 us
    add x3 -> x0, other arithmetic: 6.9 us -> none  [the longest x1 6.38 us: shards(): guess0[1:-1]]
    slice x19 -> x0, local copies, waits for them, and re-layouts: 4.27 us -> none  [the longest x8 2.23 us: tendency(): plus_y = jnp.roll(middle, -1, axis=-1)]
    unnamed x32 -> x9, local copies, waits for them, and re-layouts: 7.01 us -> 3.06 us
    pallas_call x1, Pallas kernels: 9.33 us -> 13.2 us  [run_sweep(): pl.pallas_call(functools.partial(sweep_kernel, mesh.shape['space']), out_...]
    dot_general x4, matrix products: 2.26 us -> 5.28 us  [inject(): jnp.einsum('...ay,xa->...xy', along_y, pair_table(2 * count_x), precision...]
    another operation x1 -> x0, other arithmetic: 2.14 us -> none  [shards(): return jnp.stack([node_one, node_two])[None]]
    broadcast_in_dim x1 -> x0, other arithmetic: 1.55 us -> none  [shards(): return jnp.stack([node_one, node_two])[None]]
where the time goes in v2:
time: 90.9 us; the launch traced here: 90.7 us
  Pallas kernels  72.3 us (80%)
  matrix products  14.2 us (16%)
  local copies, waits for them, and re-layouts  3.06 us (3%)
  other arithmetic  1.08 us (1%)
    pallas_call x1, Pallas kernels, run_chain(): pl.pallas_call(functools.partial(chain_kernel, count_t, count_s), out_sha...  59.1 us
    pallas_call x1, Pallas kernels, run_sweep(): pl.pallas_call(functools.partial(sweep_kernel, mesh.shape['space']), out_...  13.2 us
    dot_general x4, matrix products, inject(): jnp.einsum('...ay,xa->...xy', along_y, pair_table(2 * count_x), precision...  5.28 us
    dot_general x3, matrix products, restrict(): jnp.einsum('...xy,yb->...xb', summed_z, pair_table(count_y), precision=la...  3.83 us
    unnamed x9, local copies, waits for them, and re-layouts  3.06 us
    dot_general x4, matrix products, inject(): jnp.einsum('...ab,yb->...ay', coarse, pair_table(2 * count_y), precision=...  2.68 us
    dot_general x3, matrix products, restrict(): jnp.einsum('...xb,xa->...ab', summed_y, pair_table(count_x), precision=la...  2.38 us

profile of v2, /device:TPU:7, one launch (start us, length us, event | category | flops | bytes accessed | tf_op | source)
XLA Modules:
  0.0 90.7 jit_solution(13605897074770788217)
XLA Ops:
  0.0 0.0 copy-start
  0.0 1.7 %fusion.4 = f32[2,256,128]{2,1,0:T(8,128)S(1)} fusion(f32[2,2,256,256]{3,2,1,0:T(8,128)} %bitcast.64, s32[256]{0:T(256)S(1)} %and_select_fusion), kind=kOutput, calls=%fused_computation.13 | convolution fusion | flops 201490432 | bytes 1311744 | tf_op jit(solution)/shard_map/...xy,yb->...xb/dot_general | solution.py:28
  1.7 1.0 %fusion.source_c = f32[2,128,128]{2,1,0:T(8,128)} fusion(f32[2,256,128]{2,1,0:T(8,128)S(1)} %fusion.4, s32[256]{0:T(256)S(1)} %and_select_fusion), kind=kOutput, calls=%fused_computation.5 | convolution fusion | flops 100728832 | bytes 394240 | tf_op jit(solution)/shard_map/...xb,xa->...ab/dot_general | solution.py:31
  2.8 1.6 %fusion.8 = f32[2,256,128]{2,1,0:T(8,128)S(1)} fusion(f32[2,2,256,256]{3,2,1,0:T(8,128)} %bitcast.63, s32[256]{0:T(256)S(1)} %and_select_fusion), kind=kOutput, calls=%fused_computation.17 | convolution fusion | flops 201490432 | bytes 1311744 | tf_op jit(solution)/shard_map/...xy,yb->...xb/dot_general | solution.py:28
  4.4 1.0 %fusion.1.rate_c = f32[2,128,128]{2,1,0:T(8,128)} fusion(f32[2,256,128]{2,1,0:T(8,128)S(1)} %fusion.8, s32[256]{0:T(256)S(1)} %and_select_fusion), kind=kOutput, calls=%fused_computation.7 | convolution fusion | flops 100728832 | bytes 394240 | tf_op jit(solution)/shard_map/...xb,xa->...ab/dot_general | solution.py:31
  5.4 0.0 copy-done
  5.4 0.4 fusion.12
  5.9 0.4 fusion.2.warm_c
  6.2 0.0 copy-start.1
  6.2 0.3 fusion.31
  6.6 0.4 convolution_bitcast_fusion.3
  7.0 1.1 %bitcast_subtract_fusion.detail = f32[4,256,256]{2,1,0:T(8,128)} fusion(f32[1,4,256,256]{3,2,1,0:T(8,128)S(1)} %copy-done, f32[2,256,256]{2,1,0:T(8,128)S(1)} %convolution_bitcast_fusion.3), kind=kLoop, calls=%fused_computation.10 | loop fusion | flops 262144 | bytes 2621440 | tf_op jit(solution)/shard_map/sub | solution.py:393
  8.1 0.0 copy-done.1
  8.1 59.1 %shard_map.37 = (f32[6,256,256]{2,1,0:T(8,128)}, f32[2,256,256]{2,1,0:T(8,128)}, f32[4,128,128]{2,1,0:T(8,128)}, f32[4,128,128]{2,1,0:T(8,128)}, f32[4,128,128]{2,1,0:T(8,128)}) custom-call(f32[4,256,256]{2,1,0:T(8,128)} %bitcast_subtract_fusion.detail, f32[2,128,128]{2,1,0:T(8,128)} %copy-done.1, f32[2,128,128]{2,1,0:T(8,128)} %fusion.1.rate_c, ...), custom_call_target="tpu_custom_call" | custom-call | tf_op jit(solution)/shard_map/pallas_call | solution.py:231
  67.2 0.0 copy-start.3
  67.2 1.4 %fusion.26 = f32[4,128,256]{2,1,0:T(8,128)S(1)} fusion(f32[4,128,128]{2,1,0:T(8,128)} %get-tuple-element.12, s32[256]{0:T(256)S(1)} %and_select_fusion), kind=kOutput, calls=%fused_computation.27 | convolution fusion | flops 201359360 | bytes 787456 | tf_op jit(solution)/shard_map/...ab,yb->...ay/dot_general | solution.py:39
  68.6 0.0 copy-start.2
  68.6 1.6 %convolution_bitcast_fusion.2.start = f32[4,256,256]{2,1,0:T(8,128)} fusion(f32[4,128,256]{2,1,0:T(8,128)S(1)} %fusion.26, s32[256]{0:T(256)S(1)} %and_select_fusion), kind=kOutput, calls=%fused_computation.2 | convolution fusion | flops 402685952 | bytes 1573888 | tf_op jit(solution)/shard_map/...ay,xa->...xy/dot_general | solution.py:42
  70.2 0.0 copy-done.3
  70.2 0.5 fusion.23
  70.7 1.7 %convolution_bitcast_fusion.1.first = f32[4,256,256]{2,1,0:T(8,128)} fusion(f32[4,128,256]{2,1,0:T(8,128)S(1)} %fusion.23, s32[256]{0:T(256)S(1)} %and_select_fusion), kind=kOutput, calls=%fused_computation.1 | convolution fusion | flops 402685952 | bytes 1573888 | tf_op jit(solution)/shard_map/...ay,xa->...xy/dot_general | solution.py:42
  72.3 0.0 copy-done.2
  72.3 0.5 fusion.20
  72.8 1.6 %convolution_bitcast_fusion.second = f32[4,256,256]{2,1,0:T(8,128)} fusion(f32[4,128,256]{2,1,0:T(8,128)S(1)} %fusion.20, s32[256]{0:T(256)S(1)} %and_select_fusion), kind=kOutput, calls=%fused_computation | convolution fusion | flops 402685952 | bytes 1573888 | tf_op jit(solution)/shard_map/...ay,xa->...xy/dot_general | solution.py:42
  74.4 13.2 %shard_map.38 = f32[2,4,256,256]{3,2,1,0:T(8,128)} custom-call(f32[4,256,256]{2,1,0:T(8,128)} %bitcast_subtract_fusion.detail, f32[2,256,256]{2,1,0:T(8,128)} %get-tuple-element.10.halo, f32[6,256,256]{2,1,0:T(8,128)} %get-tuple-element.11.seed_detail, f32[4,256,256]{2,1,0:T(8,128)} %convolution_bitcast_fusion.2.start, ...), custom_call_target="tpu_custom_call" | custom-call | tf_op jit(solution)/shard_map/pallas_call | solution.py:373
  87.7 3.0 %copy.14 = f32[1,2,4,256,256]{4,3,2,1,0:T(8,128)} copy(f32[1,2,4,256,256]{4,3,2,1,0:T(8,128)} %bitcast.62) | data formatting | bytes 4194304
  (1 shorter events, 0.0 us)
Async XLA Ops:
  0.0 5.4 %copy-start = (f32[1,4,256,256]{3,2,1,0:T(8,128)S(1)}, f32[1,4,256,256]{3,2,1,0:T(8,128)}, u32[]{:S(2)}) copy-start(f32[1,4,256,256]{3,2,1,0:T(8,128)} %param.3) | copy-start | bytes 3145732
  6.2 1.8 %copy-start.1 = (f32[2,128,128]{2,1,0:T(8,128)}, f32[2,128,128]{2,1,0:T(8,128)S(1)}, u32[]{:S(2)}) copy-start(f32[2,128,128]{2,1,0:T(8,128)S(1)} %fusion.2.warm_c) | copy-start | bytes 393220
  67.2 3.1 %copy-start.3 = (f32[4,128,128]{2,1,0:T(8,128)S(1)}, f32[4,128,128]{2,1,0:T(8,128)}, u32[]{:S(2)}) copy-start(f32[4,128,128]{2,1,0:T(8,128)} %get-tuple-element.13) | copy-start | bytes 786436
  68.6 3.7 %copy-start.2 = (f32[4,128,128]{2,1,0:T(8,128)S(1)}, f32[4,128,128]{2,1,0:T(8,128)}, u32[]{:S(2)}) copy-start(f32[4,128,128]{2,1,0:T(8,128)} %get-tuple-element.14) | copy-start | bytes 786436

commit v3 on v2

--- a/solution.py
+++ b/solution.py
@@ -168,8 +168,10 @@
             ref[end - 1 : end] = jnp.zeros((1,) + ref.shape[1:], jnp.float32)
         start[2 * layers : 3 * layers] = jnp.zeros((layers,) + start.shape[1:], jnp.float32)
 
-    each(below, ups, "wait_recv")
-    each(above, downs, "wait_recv")
+    each(below, ups[0:2], "wait_recv")
+    each(above, downs[0:2], "wait_recv")
+    each(is_last & below, ups[2:3], "wait_recv")
+    each(is_last & above, downs[2:3], "wait_recv")
     each(is_last, seed_halos, "start")
 
     @pl.when(is_last)
@@ -204,13 +206,15 @@
         )
 
     going = rank < last
-    each(going, chain_next[1:2], "start")
     each(going & above, chain_next[0:1], "start")
     each(going & below, chain_next[2:3], "start")
+    each(going, chain_next[1:2], "start")
     each(above, (edge_up,), "start")
     each(below, (edge_down,), "start")
     start_out[...] = start[layers - 1 : 2 * layers + 1]
 
+    each(going & below, ups[2:3], "wait_recv")
+    each(going & above, downs[2:3], "wait_recv")
     each(going, passed, "wait_recv")
     each(leader, passed, "start")
     each(below, (edge_up,), "wait_recv")

time: 90.9 us -> 88.5 us (0.974)
  Pallas kernels: 72.3 us -> 69.6 us
    pallas_call x1, Pallas kernels: 59.1 us -> 56.3 us  [run_chain(): pl.pallas_call(functools.partial(chain_kernel, count_t, count_s), out_sha...]
where the time goes in v3:
time: 88.5 us; the launch traced here: 88 us
  Pallas kernels  69.6 us (79%)
  matrix products  14.2 us (16%)
  local copies, waits for them, and re-layouts  3.06 us (3%)
  other arithmetic  1.08 us (1%)
    pallas_call x1, Pallas kernels, run_chain(): pl.pallas_call(functools.partial(chain_kernel, count_t, count_s), out_sha...  56.3 us
    pallas_call x1, Pallas kernels, run_sweep(): pl.pallas_call(functools.partial(sweep_kernel, mesh.shape['space']), out_...  13.2 us
    dot_general x4, matrix products, inject(): jnp.einsum('...ay,xa->...xy', along_y, pair_table(2 * count_x), precision...  5.28 us
    dot_general x3, matrix products, restrict(): jnp.einsum('...xy,yb->...xb', summed_z, pair_table(count_y), precision=la...  3.83 us
    unnamed x9, local copies, waits for them, and re-layouts  3.06 us
    dot_general x4, matrix products, inject(): jnp.einsum('...ab,yb->...ay', coarse, pair_table(2 * count_y), precision=...  2.68 us
    dot_general x3, matrix products, restrict(): jnp.einsum('...xb,xa->...ab', summed_y, pair_table(count_x), precision=la...  2.38 us

profile of v3, /device:TPU:7, one launch (start us, length us, event | category | flops | bytes accessed | tf_op | source)
XLA Modules:
  0.0 88.0 jit_solution(6372594462969019344)
XLA Ops:
  0.0 0.0 copy-start
  0.0 1.7 %fusion.4 = f32[2,256,128]{2,1,0:T(8,128)S(1)} fusion(f32[2,2,256,256]{3,2,1,0:T(8,128)} %bitcast.64, s32[256]{0:T(256)S(1)} %and_select_fusion), kind=kOutput, calls=%fused_computation.13 | convolution fusion | flops 201490432 | bytes 1311744 | tf_op jit(solution)/shard_map/...xy,yb->...xb/dot_general | solution.py:28
  1.7 1.0 %fusion.source_c = f32[2,128,128]{2,1,0:T(8,128)} fusion(f32[2,256,128]{2,1,0:T(8,128)S(1)} %fusion.4, s32[256]{0:T(256)S(1)} %and_select_fusion), kind=kOutput, calls=%fused_computation.5 | convolution fusion | flops 100728832 | bytes 394240 | tf_op jit(solution)/shard_map/...xb,xa->...ab/dot_general | solution.py:31
  2.8 1.6 %fusion.8 = f32[2,256,128]{2,1,0:T(8,128)S(1)} fusion(f32[2,2,256,256]{3,2,1,0:T(8,128)} %bitcast.63, s32[256]{0:T(256)S(1)} %and_select_fusion), kind=kOutput, calls=%fused_computation.17 | convolution fusion | flops 201490432 | bytes 1311744 | tf_op jit(solution)/shard_map/...xy,yb->...xb/dot_general | solution.py:28
  4.4 1.0 %fusion.1.rate_c = f32[2,128,128]{2,1,0:T(8,128)} fusion(f32[2,256,128]{2,1,0:T(8,128)S(1)} %fusion.8, s32[256]{0:T(256)S(1)} %and_select_fusion), kind=kOutput, calls=%fused_computation.7 | convolution fusion | flops 100728832 | bytes 394240 | tf_op jit(solution)/shard_map/...xb,xa->...ab/dot_general | solution.py:31
  5.4 0.0 copy-done
  5.4 0.4 fusion.12
  5.9 0.4 fusion.2.warm_c
  6.2 0.0 copy-start.1
  6.2 0.3 fusion.31
  6.6 0.4 convolution_bitcast_fusion.3
  7.0 1.1 %bitcast_subtract_fusion.detail = f32[4,256,256]{2,1,0:T(8,128)} fusion(f32[1,4,256,256]{3,2,1,0:T(8,128)S(1)} %copy-done, f32[2,256,256]{2,1,0:T(8,128)S(1)} %convolution_bitcast_fusion.3), kind=kLoop, calls=%fused_computation.10 | loop fusion | flops 262144 | bytes 2621440 | tf_op jit(solution)/shard_map/sub | solution.py:397
  8.1 0.0 copy-done.1
  8.1 56.3 %shard_map.37 = (f32[6,256,256]{2,1,0:T(8,128)}, f32[2,256,256]{2,1,0:T(8,128)}, f32[4,128,128]{2,1,0:T(8,128)}, f32[4,128,128]{2,1,0:T(8,128)}, f32[4,128,128]{2,1,0:T(8,128)}) custom-call(f32[4,256,256]{2,1,0:T(8,128)} %bitcast_subtract_fusion.detail, f32[2,128,128]{2,1,0:T(8,128)} %copy-done.1, f32[2,128,128]{2,1,0:T(8,128)} %fusion.1.rate_c, ...), custom_call_target="tpu_custom_call" | custom-call | tf_op jit(solution)/shard_map/pallas_call | solution.py:235
  64.4 0.0 copy-start.3
  64.4 1.4 %fusion.26 = f32[4,128,256]{2,1,0:T(8,128)S(1)} fusion(f32[4,128,128]{2,1,0:T(8,128)} %get-tuple-element.12, s32[256]{0:T(256)S(1)} %and_select_fusion), kind=kOutput, calls=%fused_computation.27 | convolution fusion | flops 201359360 | bytes 787456 | tf_op jit(solution)/shard_map/...ab,yb->...ay/dot_general | solution.py:39
  65.9 0.0 copy-start.2
  65.9 1.6 %convolution_bitcast_fusion.2.start = f32[4,256,256]{2,1,0:T(8,128)} fusion(f32[4,128,256]{2,1,0:T(8,128)S(1)} %fusion.26, s32[256]{0:T(256)S(1)} %and_select_fusion), kind=kOutput, calls=%fused_computation.2 | convolution fusion | flops 402685952 | bytes 1573888 | tf_op jit(solution)/shard_map/...ay,xa->...xy/dot_general | solution.py:42
  67.5 0.0 copy-done.3
  67.5 0.4 fusion.23
  68.0 1.7 %convolution_bitcast_fusion.1.first = f32[4,256,256]{2,1,0:T(8,128)} fusion(f32[4,128,256]{2,1,0:T(8,128)S(1)} %fusion.23, s32[256]{0:T(256)S(1)} %and_select_fusion), kind=kOutput, calls=%fused_computation.1 | convolution fusion | flops 402685952 | bytes 1573888 | tf_op jit(solution)/shard_map/...ay,xa->...xy/dot_general | solution.py:42
  69.6 0.0 copy-done.2
  69.6 0.5 fusion.20
  70.1 1.6 %convolution_bitcast_fusion.second = f32[4,256,256]{2,1,0:T(8,128)} fusion(f32[4,128,256]{2,1,0:T(8,128)S(1)} %fusion.20, s32[256]{0:T(256)S(1)} %and_select_fusion), kind=kOutput, calls=%fused_computation | convolution fusion | flops 402685952 | bytes 1573888 | tf_op jit(solution)/shard_map/...ay,xa->...xy/dot_general | solution.py:42
  71.7 13.2 %shard_map.38 = f32[2,4,256,256]{3,2,1,0:T(8,128)} custom-call(f32[4,256,256]{2,1,0:T(8,128)} %bitcast_subtract_fusion.detail, f32[2,256,256]{2,1,0:T(8,128)} %get-tuple-element.10.halo, f32[6,256,256]{2,1,0:T(8,128)} %get-tuple-element.11.seed_detail, f32[4,256,256]{2,1,0:T(8,128)} %convolution_bitcast_fusion.2.start, ...), custom_call_target="tpu_custom_call" | custom-call | tf_op jit(solution)/shard_map/pallas_call | solution.py:377
  84.9 3.0 %copy.14 = f32[1,2,4,256,256]{4,3,2,1,0:T(8,128)} copy(f32[1,2,4,256,256]{4,3,2,1,0:T(8,128)} %bitcast.62) | data formatting | bytes 4194304
  (1 shorter events, 0.0 us)
Async XLA Ops:
  0.0 5.4 %copy-start = (f32[1,4,256,256]{3,2,1,0:T(8,128)S(1)}, f32[1,4,256,256]{3,2,1,0:T(8,128)}, u32[]{:S(2)}) copy-start(f32[1,4,256,256]{3,2,1,0:T(8,128)} %param.3) | copy-start | bytes 3145732
  6.2 1.8 %copy-start.1 = (f32[2,128,128]{2,1,0:T(8,128)}, f32[2,128,128]{2,1,0:T(8,128)S(1)}, u32[]{:S(2)}) copy-start(f32[2,128,128]{2,1,0:T(8,128)S(1)} %fusion.2.warm_c) | copy-start | bytes 393220
  64.4 3.1 %copy-start.3 = (f32[4,128,128]{2,1,0:T(8,128)S(1)}, f32[4,128,128]{2,1,0:T(8,128)}, u32[]{:S(2)}) copy-start(f32[4,128,128]{2,1,0:T(8,128)} %get-tuple-element.13) | copy-start | bytes 786436
  65.9 3.7 %copy-start.2 = (f32[4,128,128]{2,1,0:T(8,128)S(1)}, f32[4,128,128]{2,1,0:T(8,128)}, u32[]{:S(2)}) copy-start(f32[4,128,128]{2,1,0:T(8,128)} %get-tuple-element.14) | copy-start | bytes 786436
